TPU v7x, 32 devices: a whole 2x2x4 slice. The times are simulated.
32 devices in a mesh: seq: 16 (over z, y, x), rep: 2 (over core).
Axes of the slice: x: 2, y: 2, z: 4, core: 2. Of those that a mesh axis runs over, the one named last changes fastest.
Arguments:
- q_lin: bfloat16 [2, 2048, 4096], P('rep', 'seq'), may hold values from -90 to 90, as said below
- k_lin: bfloat16 [2, 2048, 512], P('rep', 'seq'), may hold values from -4 to 4
- value_projection: bfloat16 [2, 2048, 512], P('rep', 'seq'), may hold values from -6 to 6
- grad_out: bfloat16 [2, 2048, 4096], P('rep', 'seq'), may hold values from -6 to 6
- q_bias: float32 [4096], replicated, may hold values from -3 to 3
- block_lists: int32 [32, 16, 2], replicated, may hold values from 0 to 15, as said below
- block_counts: int32 [32, 16], replicated, may hold values from 1 to 2, as said below
Outputs:
- dq: bfloat16 [2, 2048, 4096], P('rep', 'seq')
- dk: bfloat16 [2, 2048, 512], P('rep', 'seq')
- dv: bfloat16 [2, 2048, 512], P('rep', 'seq')
- dbq: float32 [4096], replicated
Inputs may be any that keep to these rules, and one draw needn't show every extreme that they name: `q_lin`: in the shown and hidden draws alike the entries stay within the stated range. `block_lists`: entry 0 of every list is the query block itself; the 2 entries of a list are distinct; entries past block_counts are ignored. `block_counts`: some head has 2 for every query block.
All inputs are finite; a program needn't handle non-finite values.
Results may differ from a plain program's by a relative error of at most 0.008.
Values may be sent and summed in bfloat16 or wider, within the bound.
A program may use at most 128 MiB of HBM per device.

v0:
```python
import functools

import jax
import jax.numpy as jnp
from jax import lax
from jax.experimental import pallas as pl
from jax.experimental.pallas import tpu as pltpu
from jax.sharding import PartitionSpec as P

NT = (((1,), (1,)), ((), ()))
TN = (((0,), (0,)), ((), ()))
NN = (((1,), (0,)), ((), ()))


def dot(a, b, dims):
    return lax.dot_general(a, b, dims, preferred_element_type=jnp.float32)


def attend_kernel(
    head_dim, group, scaling,
    other_ref, count_ref,
    q_ref, g_ref, bias_ref, k_ref, v_ref, kall_ref, vall_ref,
    dq_ref, part_k_ref, part_v_ref, own_k_ref, own_v_ref, dbq_ref,
    acc_k, acc_v,
):
    step = pl.program_id(0)
    acc_k[...] = jnp.zeros_like(acc_k)
    acc_v[...] = jnp.zeros_like(acc_v)

    def finish(columns, grad_q):
        dq_ref[:, columns] = grad_q.astype(jnp.bfloat16)
        dbq_ref[:, columns] = jnp.sum(grad_q, axis=0, keepdims=True)

    def rows(columns):
        queries = (q_ref[:, columns].astype(jnp.float32) + bias_ref[:, columns]).astype(
            jnp.bfloat16
        )
        return queries, g_ref[:, columns]

    own_k = own_v = None
    for member in range(group):
        columns = slice(member * head_dim, (member + 1) * head_dim)
        alone = jnp.where(count_ref[step * group + member] == 1, 1.0, 0.0)
        queries, grads = rows(columns)
        keys, values = k_ref[...], v_ref[...]
        scores = dot(keys, queries, NT) * scaling
        weights = jnp.exp(scores - jnp.max(scores, axis=0, keepdims=True))
        weights = weights * (alone / jnp.sum(weights, axis=0, keepdims=True))
        half = weights.astype(jnp.bfloat16)
        weight_grads = dot(values, grads, NT)
        row_dots = jnp.sum(half.astype(jnp.float32) * weight_grads, axis=0, keepdims=True)
        score_grads = (weights * (weight_grads - row_dots)).astype(jnp.bfloat16)
        finish(columns, scaling * dot(score_grads, keys, TN))
        more_k, more_v = dot(score_grads, queries, NN), dot(half, grads, NN)
        own_k = more_k if own_k is None else own_k + more_k
        own_v = more_v if own_v is None else own_v + more_v
    own_k_ref[...] = own_k
    own_v_ref[...] = own_v

    for member in range(group):
        head = step * group + member
        columns = slice(member * head_dim, (member + 1) * head_dim)
        count = count_ref[head]
        other = other_ref[head]

        @pl.when(count != 1)
        def _():
            queries, grads = rows(columns)
            keys = [k_ref[...], kall_ref[other]]
            values = [v_ref[...], vall_ref[other]]
            scores = [dot(one, queries, NT) * scaling for one in keys]
            top = jnp.maximum(
                jnp.max(scores[0], axis=0, keepdims=True), jnp.max(scores[1], axis=0, keepdims=True)
            )
            weights = [jnp.exp(one - top) for one in scores]
            total = jnp.sum(weights[0], axis=0, keepdims=True) + jnp.sum(
                weights[1], axis=0, keepdims=True
            )
            scale_to = 1.0 / total
            weights = [one * scale_to for one in weights]
            half = [one.astype(jnp.bfloat16) for one in weights]
            weight_grads = [dot(one, grads, NT) for one in values]
            row_dots = sum(
                jnp.sum(a.astype(jnp.float32) * b, axis=0, keepdims=True)
                for a, b in zip(half, weight_grads)
            )
            score_grads = [
                (a * (b - row_dots)).astype(jnp.bfloat16) for a, b in zip(weights, weight_grads)
            ]
            finish(
                columns,
                scaling * (dot(score_grads[0], keys[0], TN) + dot(score_grads[1], keys[1], TN)),
            )
            own_k_ref[...] += dot(score_grads[0], queries, NN)
            own_v_ref[...] += dot(half[0], grads, NN)
            acc_k[other] += dot(score_grads[1], queries, NN)
            acc_v[other] += dot(half[1], grads, NN)

    own_k_ref[...] = own_k_ref[...] * scaling
    part_k_ref[...] = (acc_k[...] * scaling).astype(jnp.bfloat16)
    part_v_ref[...] = acc_v[...].astype(jnp.bfloat16)


def attend(q, g, bias, k, v, kall, vall, other, count):
    rows, width = q.shape
    blocks = kall.shape[0]
    heads = other.shape[0]
    head_dim = width // heads
    kv_count = k.shape[1] // head_dim
    group = heads // kv_count
    wide = pl.BlockSpec((rows, group * head_dim), lambda s, *_: (0, s))
    thin = pl.BlockSpec((rows, head_dim), lambda s, *_: (0, s))
    line = pl.BlockSpec((1, group * head_dim), lambda s, *_: (0, s))
    whole = pl.BlockSpec((blocks, rows, head_dim), lambda s, *_: (0, 0, s))
    return pl.pallas_call(
        functools.partial(attend_kernel, head_dim, group, head_dim ** (-0.5)),
        grid_spec=pltpu.PrefetchScalarGridSpec(
            num_scalar_prefetch=2,
            grid=(kv_count,),
            in_specs=[wide, wide, line, thin, thin, whole, whole],
            out_specs=[wide, whole, whole, thin, thin, line],
            scratch_shapes=[
                pltpu.VMEM((blocks, rows, head_dim), jnp.float32),
                pltpu.VMEM((blocks, rows, head_dim), jnp.float32),
            ],
        ),
        out_shape=[
            jax.ShapeDtypeStruct((rows, width), jnp.bfloat16),
            jax.ShapeDtypeStruct(kall.shape, jnp.bfloat16),
            jax.ShapeDtypeStruct(vall.shape, jnp.bfloat16),
            jax.ShapeDtypeStruct(k.shape, jnp.float32),
            jax.ShapeDtypeStruct(v.shape, jnp.float32),
            jax.ShapeDtypeStruct((1, width), jnp.float32),
        ],
        compiler_params=pltpu.CompilerParams(vmem_limit_bytes=56 * 1024 * 1024),
        name="attend",
    )(other, count, q, g, bias, k, v, kall, vall)


MESH = pl.DeviceIdType.MESH


def place():
    me = lax.axis_index("seq")
    n = lax.axis_size("seq")
    lines = n // 4
    z, p = me // 4, me % 4
    x, y = p % 2, p // 2
    px = y * 2 + (1 - x)
    py = (1 - y) * 2 + x
    far = (1 - y) * 2 + (1 - x)
    return lines, z, p, px, py, far


def greet(targets, extra=()):
    barrier = pltpu.get_barrier_semaphore()
    for target in targets:
        pl.semaphore_signal(barrier, inc=1, device_id={"seq": target}, device_id_type=MESH)
    for target in extra:
        pl.semaphore_signal(barrier, inc=1, device_id={"rep": target}, device_id_type=MESH)
    pl.semaphore_wait(barrier, len(targets) + len(extra))


class Sender:
    def __init__(self, send_sem, recv_sem):
        self.send_sem, self.recv_sem, self.next, self.open = send_sem, recv_sem, 0, []

    def __call__(self, src, dst, **target):
        copy = pltpu.make_async_remote_copy(
            src_ref=src,
            dst_ref=dst,
            send_sem=self.send_sem.at[self.next],
            recv_sem=self.recv_sem.at[self.next],
            device_id=target,
            device_id_type=MESH,
        )
        self.next += 1
        copy.start()
        self.open.append(copy)
        return copy

    def drain(self):
        for copy in self.open:
            copy.wait_send()


def gather_kernel(k_ref, v_ref, kall_ref, vall_ref, send_sem, recv_sem, local_sem):
    lines, z, p, px, py, far = place()
    me = z * 4 + p
    zs = [lax.rem(z + lines - d, lines) for d in range(lines)]
    up = [lax.rem(z + d, lines) for d in range(lines)]
    greet([up[d] * 4 + p for d in range(1, lines)] + [z * 4 + px, z * 4 + py])
    send = Sender(send_sem, recv_sem)
    arrays = [(k_ref, kall_ref, px, py), (v_ref, vall_ref, py, px)]
    along, first, last = {}, {}, []
    own = []
    for a, (src, out, f, s) in enumerate(arrays):
        own.append(pltpu.make_async_copy(src, out.at[me], local_sem.at[a]))
        own[-1].start()
    for d in range(1, lines):
        for a, (src, out, f, s) in enumerate(arrays):
            along[a, d] = send(src, out.at[me], seq=up[d] * 4 + p)
    for d in range(lines + 1):
        if d < lines:
            for a, (src, out, f, s) in enumerate(arrays):
                spot = zs[d] * 4 + p
                if d:
                    along[a, d].wait_recv()
                piece = out.at[spot] if d else src
                first[a, d] = send(piece, out.at[spot], seq=z * 4 + f)
            for a, (src, out, f, s) in enumerate(arrays):
                spot = zs[d] * 4 + p
                piece = out.at[spot] if d else src
                last.append(send(piece, out.at[spot], seq=z * 4 + s))
        if d:
            for a, (src, out, f, s) in enumerate(arrays):
                spot = zs[d - 1] * 4 + f
                first[a, d - 1].wait_recv()
                last.append(send(out.at[spot], out.at[spot], seq=z * 4 + s))
    for copy in last:
        copy.wait_recv()
    send.drain()
    for copy in own:
        copy.wait()


def gather(k, v):
    n = lax.axis_size("seq")
    assert n % 4 == 0
    copies = 2 * (n // 4 - 1 + 3 * (n // 4))
    spec = pl.BlockSpec(memory_space=pl.ANY)
    return pl.pallas_call(
        gather_kernel,
        in_specs=[spec, spec],
        out_specs=[spec, spec],
        out_shape=[jax.ShapeDtypeStruct((n,) + one.shape, one.dtype) for one in (k, v)],
        scratch_shapes=[
            pltpu.SemaphoreType.DMA((copies,)),
            pltpu.SemaphoreType.DMA((copies,)),
            pltpu.SemaphoreType.DMA((2,)),
        ],
        compiler_params=pltpu.CompilerParams(collective_id=1, has_side_effects=True),
        name="gather",
    )(k, v)


def scatter_kernel(
    part_k, part_v, own_k, own_v, bias_ref,
    dk_ref, dv_ref, dbq_ref,
    half_k, half_v, line_k, line_v, end_k, end_v,
    rep_slots, x_slots, y_slots, z_slots, sums, send_sem, recv_sem,
):
    lines, z, p, px, py, far = place()
    me = z * 4 + p
    reps, rep = lax.axis_size("rep"), lax.axis_index("rep")
    up = [lax.rem(z + d, lines) for d in range(lines)]
    others = [lax.rem(rep + d, reps) for d in range(1, reps)]
    greet([up[d] * 4 + p for d in range(1, lines)] + [z * 4 + px, z * 4 + py], others)
    send = Sender(send_sem, recv_sem)
    arrays = [
        (part_k, own_k, dk_ref, half_k, line_k, end_k, px, py),
        (part_v, own_v, dv_ref, half_v, line_v, end_v, py, px),
    ]
    order = list(range(1, lines)) + [0]

    rep_slots[rep] = bias_ref[...]
    bias = [send(bias_ref, rep_slots.at[rep], rep=other) for other in others]
    x, y = p % 2, p // 2
    near, cross, down, ends = {}, {}, {}, []

    def open_step(j):
        if j >= lines:
            return
        d = order[j]
        for a, (part, own, out, half, line, end, f, s) in enumerate(arrays):
            cross[a, d] = send(part.at[up[d] * 4 + far], half.at[d, 1], seq=z * 4 + s)
        for a, (part, own, out, half, line, end, f, s) in enumerate(arrays):
            near[a, d] = send(part.at[up[d] * 4 + s], half.at[d, 0], seq=z * 4 + s)

    open_step(0)

    def total(slots, count):
        result = slots[0]
        for j in range(1, count):
            result = result + slots[j]
        return result

    def relay(stage):
        nonlocal bias
        for copy in bias:
            copy.wait_recv()
        if stage == 0:
            sums[0] = total(rep_slots, reps)
            x_slots[x] = sums[0]
            bias = [send(sums.at[0], x_slots.at[x], seq=z * 4 + px)]
        elif stage == 1:
            sums[1] = total(x_slots, 2)
            y_slots[y] = sums[1]
            bias = [send(sums.at[1], y_slots.at[y], seq=z * 4 + py)]
        elif stage == 2:
            sums[2] = total(y_slots, 2)
            z_slots[z] = sums[2]
            bias = [
                send(sums.at[2], z_slots.at[z], seq=up[d] * 4 + p) for d in range(1, lines)
            ]
        else:
            dbq_ref[...] = total(z_slots, lines)

    stage = 0
    for j in range(lines + 1):
        if j < lines:
            open_step(j + 1)
            d = order[j]
            for a, (part, own, out, half, line, end, f, s) in enumerate(arrays):
                cross[a, d].wait_recv()
                half[d, 1] = half[d, 1] + part[up[d] * 4 + f]
                down[a, d] = send(half.at[d, 1], line.at[d], seq=z * 4 + f)
            for a, (part, own, out, half, line, end, f, s) in enumerate(arrays):
                near[a, d].wait_recv()
        if stage < 3:
            relay(stage)
            stage += 1
        if j:
            d = order[j - 1]
            for a, (part, own, out, half, line, end, f, s) in enumerate(arrays):
                down[a, d].wait_recv()
                summed = (
                    half[d, 0].astype(jnp.float32)
                    + part[up[d] * 4 + p].astype(jnp.float32)
                    + line[d].astype(jnp.float32)
                )
                if d:
                    line[d] = summed.astype(jnp.bfloat16)
                    ends.append((a, d, send(line.at[d], end.at[d - 1], seq=up[d] * 4 + p)))
                else:
                    line[d] = summed.astype(jnp.bfloat16)
    while stage < 4:
        relay(stage)
        stage += 1
    for a, d, copy in ends:
        copy.wait_recv()
    for part, own, out, half, line, end, f, s in arrays:
        result = own[...] + line[0].astype(jnp.float32)
        for d in range(lines - 1):
            result = result + end[d].astype(jnp.float32)
        out[...] = result.astype(jnp.bfloat16)
    send.drain()


def scatter(part_k, part_v, own_k, own_v, bias):
    n, reps = lax.axis_size("seq"), lax.axis_size("rep")
    lines = n // 4
    block, kind = part_k.shape[1:], part_k.dtype
    copies = 2 * (4 * lines - 1) + (reps - 1) + 2 + (lines - 1)
    spec = pl.BlockSpec(memory_space=pltpu.VMEM)
    slots = [reps, 2, 2, lines, 3]
    return pl.pallas_call(
        scatter_kernel,
        in_specs=[spec] * 5,
        out_specs=[spec] * 3,
        out_shape=[
            jax.ShapeDtypeStruct(block, kind),
            jax.ShapeDtypeStruct(block, kind),
            jax.ShapeDtypeStruct(bias.shape, jnp.float32),
        ],
        scratch_shapes=[pltpu.VMEM((lines, 2) + block, kind)] * 2
        + [pltpu.VMEM((lines,) + block, kind)] * 2
        + [pltpu.VMEM((lines - 1,) + block, kind)] * 2
        + [pltpu.VMEM((count,) + bias.shape, jnp.float32) for count in slots]
        + [pltpu.SemaphoreType.DMA((copies,))] * 2,
        compiler_params=pltpu.CompilerParams(
            collective_id=2, has_side_effects=True, vmem_limit_bytes=60 * 1024 * 1024
        ),
        name="scatter",
    )(part_k, part_v, own_k, own_v, bias)


def body(q_lin, k_lin, value_projection, grad_out, q_bias, block_lists, block_counts):
    me = lax.axis_index("seq")
    assert block_lists.shape[1] == lax.axis_size("seq") and block_lists.shape[2] == 2
    lists = lax.dynamic_index_in_dim(block_lists, me, 1, keepdims=False)
    count = lax.dynamic_index_in_dim(block_counts, me, 1, keepdims=False)
    other = jnp.clip(lists[:, 1], 0, block_lists.shape[1] - 1)
    kall, vall = gather(k_lin[0], value_projection[0])
    dq, part_k, part_v, own_k, own_v, dbq = attend(
        q_lin[0], grad_out[0], q_bias[None], k_lin[0], value_projection[0], kall, vall, other, count
    )
    dk, dv, dbq = scatter(part_k, part_v, own_k, own_v, dbq)
    return (dq[None], dk[None], dv[None], dbq.reshape(-1))


def solution(mesh):
    placed = (P("rep", "seq", None),) * 4 + (P(),) * 3
    return jax.shard_map(
        body,
        mesh=mesh,
        in_specs=placed,
        out_specs=(P("rep", "seq", None),) * 3 + (P(),),
        check_vma=False,
    )
```

profile of v0, /device:TPU:0, one launch (start us, length us, event | category | flops | bytes accessed | tf_op | source)
XLA Modules:
  0.0 121.8 jit_solution(1336702307811274118)
XLA Ops:
  0.6 0.0 copy-start
  0.6 0.7 copy-done
  1.4 1.2 dynamic-slice_bitcast_fusion.1
  2.6 45.4 %gather.1 = (bf16[16,128,512]{2,1,0:T(8,128)(2,1)}, bf16[16,128,512]{2,1,0:T(8,128)(2,1)}) custom-call(bf16[128,512]{1,0:T(8,128)(2,1)} %bitcast.17, bf16[128,512]{1,0:T(8,128)(2,1)} %bitcast.19), custom_call_target="tpu_custom_call" | custom-call | tf_op jit(solution)/shard_map/gather/pallas_call | solution.py:232
  47.9 17.8 %attend.1 = (bf16[128,4096]{1,0:T(8,128)(2,1)}, bf16[16,128,512]{2,1,0:T(8,128)(2,1)}, bf16[16,128,512]{2,1,0:T(8,128)(2,1)}, f32[128,512]{1,0:T(8,128)}, f32[128,512]{1,0:T(8,128)}, /*index=5*/f32[1,4096]{1,0:T(1,128)}) custom-call(s32[32]{0:T(128)} %get-tuple-element.27.other_ref, s32[32]{0:T(128)} %get-tuple-element.26.count_ref, ...), custom_call_target="tpu_custom_call" | custom-call | tf_op jit(solution)/shard_map/attend/pallas_call | solution.py:115
  65.7 51.6 %scatter.1 = (bf16[128,512]{1,0:T(8,128)(2,1)}, bf16[128,512]{1,0:T(8,128)(2,1)}, f32[1,4096]{1,0:T(1,128)}) custom-call(bf16[16,128,512]{2,1,0:T(8,128)(2,1)} %get-tuple-element.18.part_k, bf16[16,128,512]{2,1,0:T(8,128)(2,1)} %get-tuple-element.19.part_v, f32[128,512]{1,0:T(8,128)} %get-tuple-element.20.own_k, f32[128,512]{1,0:T(8,128)} %get-tuple-element.21.own_v, ...), custom_call_target="tpu_custom_call" | custom-call | tf_op jit(solution)/shard_map/scatter/pallas_call | solution.py:357
  117.4 1.6 %copy.14 = bf16[1,128,512]{2,1,0:T(8,128)(2,1)} copy(bf16[1,128,512]{2,1,0:T(8,128)(2,1)} %bitcast.22) | data formatting | bytes 262144
  118.9 1.6 %copy.15 = bf16[1,128,512]{2,1,0:T(8,128)(2,1)} copy(bf16[1,128,512]{2,1,0:T(8,128)(2,1)} %bitcast.21) | data formatting | bytes 262144
  120.5 1.3 %copy.16 = f32[4096]{0:T(1024)} copy(f32[4096]{0:T(1024)} %bitcast.24) | data formatting | bytes 32768
  (1 shorter events, 0.0 us)
Async XLA Ops:
  0.6 0.7 copy-start
where the time goes:
time: 123 us; the launch traced here: 122 us
  Pallas kernels  115 us (93%)
  local copies, waits for them, and re-layouts  5.17 us (4%)
    pallas_call x1, Pallas kernels, scatter(): pl.pallas_call(scatter_kernel, in_specs=[spec] * 5, out_specs=[spec] * 3,...  51.6 us
    pallas_call x1, Pallas kernels, gather(): pl.pallas_call(gather_kernel, in_specs=[spec, spec], out_specs=[spec, spe...  45.4 us
    pallas_call x1, Pallas kernels, attend(): pl.pallas_call(functools.partial(attend_kernel, head_dim, group, head_dim...  17.8 us
    unnamed x5, local copies, waits for them, and re-layouts  5.17 us

commit v1 on v0

v1 whole, which is shorter than its diff:
```python
import functools

import jax
import jax.numpy as jnp
from jax import lax
from jax.experimental import pallas as pl
from jax.experimental.pallas import tpu as pltpu
from jax.sharding import PartitionSpec as P

NT = (((1,), (1,)), ((), ()))
TN = (((0,), (0,)), ((), ()))
NN = (((1,), (0,)), ((), ()))
MESH = pl.DeviceIdType.MESH
PLANE = 4
UNROLL = 4


def dot(a, b, dims):
    return lax.dot_general(a, b, dims, preferred_element_type=jnp.float32)


def fused_kernel(
    group, scaling,
    lists_ref, count_ref, bias_ref, q_ref, g_ref, k_ref, v_ref,
    dq_ref, dk_ref, dv_ref, dbq_ref,
    kall, vall, qbuf, gbuf, dqbuf, weights_buf, chain_k, chain_v, own_k, own_v,
    rs_send, rs_recv, final, bias_acc, rep_slots, z_slots, bias_sums,
    enc_ref, prev_ref, last_ref,
    local_sem, plane_send, plane_recv, rows_send, rows_recv, z_send, z_recv,
    dq_local, dq_send, dq_recv, rs_send_sem, rs_recv_sem,
    out_local, out_send, out_recv, rep_send, rep_recv, zb_send, zb_recv, pb_send, pb_recv,
):
    me = lax.axis_index("seq")
    n = lax.axis_size("seq")
    reps, rep = lax.axis_size("rep"), lax.axis_index("rep")
    lines = n // PLANE
    z, p = me // PLANE, me % PLANE
    rows, width = kall.shape[1:]
    halves = group // UNROLL
    steps = PLANE * halves
    piece = UNROLL * width
    pairs = PLANE * group

    def near(s):
        return (p // 2 + s // 2) % 2 * 2 + (p % 2 + s % 2) % 2

    def seq(zz, pp):
        return {"seq": zz * PLANE + pp}

    def remote(src, dst, send, recv, target):
        return pltpu.make_async_remote_copy(
            src_ref=src, dst_ref=dst, send_sem=send, recv_sem=recv,
            device_id=target, device_id_type=MESH,
        )

    def cols(start, size):
        return pl.ds(pl.multiple_of(start * width, width), size * width)

    own_kv = [
        pltpu.make_async_copy(src.at[:, cols(p, 1)], dst.at[me], local_sem.at[a])
        for a, (src, dst) in enumerate([(k_ref, kall), (v_ref, vall)])
    ]
    own_rows = [
        pltpu.make_async_copy(
            src.at[:, cols(p * group + hb * UNROLL, UNROLL)], dst.at[hb],
            local_sem.at[2 + a * halves + hb],
        )
        for a, (src, dst) in enumerate([(q_ref, qbuf), (g_ref, gbuf)])
        for hb in range(halves)
    ]
    for copy in own_kv + own_rows:
        copy.start()

    barrier = pltpu.get_barrier_semaphore()
    z_others = [lax.rem(z + d, lines) for d in range(1, lines)]
    rep_others = [lax.rem(rep + d, reps) for d in range(1, reps)]
    for s in range(1, PLANE):
        pl.semaphore_signal(barrier, inc=1, device_id=seq(z, near(s)), device_id_type=MESH)
    for zz in z_others:
        pl.semaphore_signal(barrier, inc=1, device_id=seq(zz, p), device_id_type=MESH)
    for rr in rep_others:
        pl.semaphore_signal(barrier, inc=1, device_id={"rep": rr}, device_id_type=MESH)
    pl.semaphore_wait(barrier, PLANE - 1 + lines - 1 + reps - 1)

    def plane_copy(a, s):
        src, dst = [(k_ref, kall), (v_ref, vall)][a]
        return remote(
            src.at[:, cols(near(s), 1)], dst.at[me],
            plane_send.at[a, s - 1], plane_recv.at[a, s - 1], seq(z, near(s)),
        )

    for a in range(2):
        for s in range(1, PLANE):
            plane_copy(a, s).start()

    def rows_copy(a, it):
        s, hb = it // halves, it % halves
        src, dst = [(q_ref, qbuf), (g_ref, gbuf)][a]
        return remote(
            src.at[:, cols(near(s) * group + hb * UNROLL, UNROLL)], dst.at[it],
            rows_send.at[a, it], rows_recv.at[a, it], seq(z, near(s)),
        )

    for a in range(2):
        for it in range(halves, steps):
            rows_copy(a, it).start()

    def z_copy(a, way, d):
        dst = [kall, vall][a]
        block = dst.at[pl.ds((z - d if way == 0 else z + d) * PLANE, PLANE)]
        return remote(
            block, block, z_send.at[a, way, d], z_recv.at[a, way, d],
            seq(z + 1 if way == 0 else z - 1, p),
        )

    def z_start(a, d):
        @pl.when((z + 1 < lines) & (z - d >= 0))
        def _():
            z_copy(a, 0, d).start()

        @pl.when((z - 1 >= 0) & (z + d < lines))
        def _():
            z_copy(a, 1, d).start()

    def z_arrive(a, d):
        dst = [kall, vall][a]

        def arrived(way, where):
            block = dst.at[pl.ds(where * PLANE, PLANE)]
            remote(
                block, block, z_send.at[a, way, d - 1], z_recv.at[a, way, d - 1], seq(z, p)
            ).wait_recv()

        @pl.when(z - d >= 0)
        def _():
            arrived(0, z - d)

        @pl.when(z + d < lines)
        def _():
            arrived(1, z + d)

    def z_open(a):
        own_kv[a].wait()
        for s in range(1, PLANE):
            plane_copy(a, s).wait_recv()
        z_start(a, 0)

    def z_relay(a, d):
        z_arrive(a, d)
        if d < lines - 1:
            z_start(a, d)

    def read_table(t, _):
        s, h = t // group, t % group
        position = z * PLANE + near(s)
        head = p * group + h
        other = jnp.clip(lists_ref[position, 1, head], 0, n - 1)
        enc_ref[t] = jnp.where(count_ref[position, head] != 1, other, n)
        return 0

    lax.fori_loop(0, pairs, read_table, 0)

    z_open(0)

    def link_pair(t, _):
        code = enc_ref[t]
        found = jnp.int32(0)
        for u in range(pairs):
            same = (enc_ref[u] == code) & (u < t)
            found = jnp.where(same, u + 1, found)
        prev_ref[t] = found
        return 0

    lax.fori_loop(0, pairs, link_pair, 0)
    z_open(1)

    def link_block(j, _):
        found = jnp.int32(0)
        for u in range(pairs):
            found = jnp.where(enc_ref[u] == j, u + 1, found)
        last_ref[j] = found
        return 0

    lax.fori_loop(0, n, link_block, 0)

    chain_k[0] = jnp.zeros((rows, width), jnp.float32)
    chain_v[0] = jnp.zeros((rows, width), jnp.float32)
    own_k[...] = jnp.zeros_like(own_k)
    own_v[...] = jnp.zeros_like(own_v)
    bias_acc[...] = jnp.zeros_like(bias_acc)

    for d in range(1, lines):
        z_relay(0, d)
    for copy in own_rows:
        copy.wait()

    def both(ref, it, u):
        t = it * UNROLL + u
        code = enc_ref[t]
        other = jnp.where(code < n, code, 0)
        position = z * PLANE + near(it // halves)
        return jnp.concatenate([ref[position], ref[other]], axis=0), code

    def soften(it, _):
        @pl.when(it >= halves)
        def _():
            rows_copy(0, it).wait_recv()

        for u in range(UNROLL):
            lanes = slice(u * width, (u + 1) * width)
            head = p * group + (it % halves) * UNROLL + u
            queries = (
                qbuf[it, :, lanes].astype(jnp.float32) + bias_ref[pl.ds(head, 1), :]
            ).astype(jnp.bfloat16)
            qbuf[it, :, lanes] = queries
            keys, code = both(kall, it, u)
            scores = dot(keys, queries, NT) * scaling
            first = scores[:rows]
            second = scores[rows:] + jnp.where(code < n, 0.0, -1.0e30)
            top = jnp.maximum(
                jnp.max(first, axis=0, keepdims=True), jnp.max(second, axis=0, keepdims=True)
            )
            first, second = jnp.exp(first - top), jnp.exp(second - top)
            total = jnp.sum(first, axis=0, keepdims=True) + jnp.sum(second, axis=0, keepdims=True)
            scale_to = 1.0 / total
            weights_buf[it * UNROLL + u, :rows] = first * scale_to
            weights_buf[it * UNROLL + u, rows:] = second * scale_to
        return 0

    def dq_copy(it):
        s, hb = it // halves, it % halves
        return remote(
            dqbuf.at[it], dq_ref.at[:, cols(p * group + hb * UNROLL, UNROLL)],
            dq_send.at[it], dq_recv.at[it], seq(z, near(s)),
        )

    def dq_stay(it):
        return pltpu.make_async_copy(
            dqbuf.at[it], dq_ref.at[:, cols(p * group + it * UNROLL, UNROLL)], dq_local.at[it]
        )

    def dq_arrive(it):
        s, hb = it // halves, it % halves
        return remote(
            dqbuf.at[it], dq_ref.at[:, cols(near(s) * group + hb * UNROLL, UNROLL)],
            dq_send.at[it], dq_recv.at[it], seq(z, near(s)),
        )

    def differentiate(it, _):
        s = it // halves

        @pl.when(it >= halves)
        def _():
            rows_copy(1, it).wait_recv()

        more_k = more_v = None
        for u in range(UNROLL):
            t = it * UNROLL + u
            lanes = slice(u * width, (u + 1) * width)
            head = (it % halves) * UNROLL + u
            queries, grads = qbuf[it, :, lanes], gbuf[it, :, lanes]
            keys, _ = both(kall, it, u)
            values, _ = both(vall, it, u)
            weights = weights_buf[t]
            half = weights.astype(jnp.bfloat16)
            weight_grads = dot(values, grads, NT)
            row_dots = jnp.sum(half.astype(jnp.float32) * weight_grads, axis=0, keepdims=True)
            score_grads = (weights * (weight_grads - row_dots)).astype(jnp.bfloat16)
            grad_q = scaling * dot(score_grads, keys, TN)
            dqbuf[it, :, lanes] = grad_q.astype(jnp.bfloat16)
            bias_acc[pl.ds(head, 1), :] += jnp.sum(grad_q, axis=0, keepdims=True)
            part_k, part_v = dot(score_grads, queries, NN), dot(half, grads, NN)
            before = prev_ref[t]
            chain_k[t + 1] = part_k[rows:] + chain_k[before]
            chain_v[t + 1] = part_v[rows:] + chain_v[before]
            more_k = part_k[:rows] if more_k is None else more_k + part_k[:rows]
            more_v = part_v[:rows] if more_v is None else more_v + part_v[:rows]
        position = near(s)
        own_k[position] += more_k
        own_v[position] += more_v

        @pl.when(it < halves)
        def _():
            dq_stay(it).start()

        @pl.when(it >= halves)
        def _():
            dq_copy(it).start()

        return 0

    share = [steps * d // lines for d in range(lines + 1)]
    for d in range(lines):
        if d:
            z_relay(1, d)
        lax.fori_loop(share[d], share[d + 1], soften, 0)
    lax.fori_loop(0, steps, differentiate, 0)

    rep_slots[rep] = bias_acc[...]

    def rep_copy(d):
        return remote(
            bias_acc, rep_slots.at[rep], rep_send.at[d - 1], rep_recv.at[d - 1],
            {"rep": rep_others[d - 1]},
        )

    for d in range(1, reps):
        rep_copy(d).start()

    factors = [scaling, 1.0]
    chains = [chain_k, chain_v]
    owns = [own_k, own_v]

    def rs_copy(a, way, d):
        return remote(
            rs_send.at[a, way, d - 1], rs_recv.at[a, way, d - 1],
            rs_send_sem.at[a, way, d - 1], rs_recv_sem.at[a, way, d - 1],
            seq(z + 1 if way == 0 else z - 1, p),
        )

    def rs_step(a, way, d):
        target = z + d if way == 0 else z - d
        inside = target < lines if way == 0 else target >= 0
        inner = z >= 1 if way == 0 else z + 1 < lines

        def part(j):
            return chains[a][last_ref[target * PLANE + j]] * factors[a]

        if d < lines - 1:
            @pl.when(inside & inner)
            def _():
                rs_copy(a, way, d + 1).wait_recv()
                for j in range(PLANE):
                    rs_send[a, way, d - 1, j] = (
                        part(j) + rs_recv[a, way, d, j].astype(jnp.float32)
                    ).astype(jnp.bfloat16)
                rs_copy(a, way, d).start()

            inside = inside & jnp.logical_not(inner)

        @pl.when(inside)
        def _():
            for j in range(PLANE):
                rs_send[a, way, d - 1, j] = part(j).astype(jnp.bfloat16)
            rs_copy(a, way, d).start()

    rs_step(1, 0, lines - 1)
    rs_step(1, 1, lines - 1)

    for d in range(1, reps):
        rep_copy(d).wait_recv()
    summed = rep_slots[0]
    for d in range(1, reps):
        summed = summed + rep_slots[d]
    bias_sums[0] = summed
    z_slots[z] = summed

    def zb_copy(d):
        return remote(
            bias_sums.at[0], z_slots.at[z], zb_send.at[d - 1], zb_recv.at[d - 1],
            seq(z_others[d - 1], p),
        )

    for d in range(1, lines):
        zb_copy(d).start()

    for a in (1, 0):
        for d in range(lines - 1, 0, -1):
            if a == 0 or d < lines - 1:
                rs_step(a, 0, d)
                rs_step(a, 1, d)

    def out_copy(a, s):
        return remote(
            final.at[a, near(s)], [dk_ref, dv_ref][a].at[:, cols(p, 1)],
            out_send.at[a, s - 1], out_recv.at[a, s - 1], seq(z, near(s)),
        )

    def out_arrive(a, s):
        return remote(
            final.at[a, near(s)], [dk_ref, dv_ref][a].at[:, cols(near(s), 1)],
            out_send.at[a, s - 1], out_recv.at[a, s - 1], seq(z, near(s)),
        )

    def out_stay(a):
        return pltpu.make_async_copy(
            final.at[a, p], [dk_ref, dv_ref][a].at[:, cols(p, 1)], out_local.at[a]
        )

    for a in (1, 0):
        base = []
        for j in range(PLANE):
            owns[a][j] = (owns[a][j] + chains[a][last_ref[z * PLANE + j]]) * factors[a]

        for way, inner in ((0, z >= 1), (1, z + 1 < lines)):
            @pl.when(inner)
            def _():
                rs_copy(a, way, 1).wait_recv()
                for j in range(PLANE):
                    owns[a][j] += rs_recv[a, way, 0, j].astype(jnp.float32)

        for j in range(PLANE):
            final[a, j] = owns[a][j].astype(jnp.bfloat16)
        for s in (3, 1, 2):
            out_copy(a, s).start()
        out_stay(a).start()

    for d in range(1, lines):
        zb_copy(d).wait_recv()
    summed = z_slots[0]
    for d in range(1, lines):
        summed = summed + z_slots[d]
    bias_sums[1] = summed
    mine = pl.ds(pl.multiple_of(p * group, group), group)
    dbq_ref[mine, :] = summed

    def pb_copy(s):
        return remote(
            bias_sums.at[1], dbq_ref.at[mine], pb_send.at[s - 1], pb_recv.at[s - 1],
            seq(z, near(s)),
        )

    def pb_arrive(s):
        return remote(
            bias_sums.at[1],
            dbq_ref.at[pl.ds(pl.multiple_of(near(s) * group, group), group)],
            pb_send.at[s - 1], pb_recv.at[s - 1], seq(z, near(s)),
        )

    for s in range(1, PLANE):
        pb_copy(s).start()

    for a in range(2):
        for s in range(1, PLANE):
            plane_copy(a, s).wait_send()
        for it in range(halves, steps):
            rows_copy(a, it).wait_send()
        for way in range(2):
            for d in range(lines - 1):
                ahead = z + 1 < lines if way == 0 else z >= 1
                behind = z - d >= 0 if way == 0 else z + d < lines

                @pl.when(ahead & behind)
                def _():
                    z_copy(a, way, d).wait_send()

            for d in range(1, lines):
                @pl.when(z + d < lines if way == 0 else z - d >= 0)
                def _():
                    rs_copy(a, way, d).wait_send()
    for it in range(halves):
        dq_stay(it).wait()
    for it in range(halves, steps):
        dq_copy(it).wait_send()
        dq_arrive(it).wait_recv()
    for d in range(1, reps):
        rep_copy(d).wait_send()
    for d in range(1, lines):
        zb_copy(d).wait_send()
    for a in range(2):
        out_stay(a).wait()
        for s in range(1, PLANE):
            out_copy(a, s).wait_send()
            out_arrive(a, s).wait_recv()
    for s in range(1, PLANE):
        pb_copy(s).wait_send()
        pb_arrive(s).wait_recv()


def fused(lists, counts, bias, q, g, k, v):
    n, reps = lax.axis_size("seq"), lax.axis_size("rep")
    rows, total = q.shape
    heads, width = bias.shape
    kv_count = k.shape[1] // width
    group = heads // kv_count
    assert n % PLANE == 0 and kv_count == PLANE and group % UNROLL == 0
    lines = n // PLANE
    halves = group // UNROLL
    steps = PLANE * halves
    pairs = PLANE * group
    half, full = jnp.bfloat16, jnp.float32
    smem = pl.BlockSpec(memory_space=pltpu.SMEM)
    vmem = pl.BlockSpec(memory_space=pltpu.VMEM)
    free = pl.BlockSpec(memory_space=pl.ANY)
    dma = pltpu.SemaphoreType.DMA
    return pl.pallas_call(
        functools.partial(fused_kernel, group, width ** (-0.5)),
        in_specs=[smem, smem, vmem, free, free, free, free],
        out_specs=[free, free, free, vmem],
        out_shape=[
            jax.ShapeDtypeStruct(q.shape, half),
            jax.ShapeDtypeStruct(k.shape, half),
            jax.ShapeDtypeStruct(v.shape, half),
            jax.ShapeDtypeStruct(bias.shape, full),
        ],
        scratch_shapes=[
            pltpu.VMEM((n, rows, width), half),
            pltpu.VMEM((n, rows, width), half),
            pltpu.VMEM((steps, rows, UNROLL * width), half),
            pltpu.VMEM((steps, rows, UNROLL * width), half),
            pltpu.VMEM((steps, rows, UNROLL * width), half),
            pltpu.VMEM((pairs, 2 * rows, rows), full),
            pltpu.VMEM((pairs + 1, rows, width), full),
            pltpu.VMEM((pairs + 1, rows, width), full),
            pltpu.VMEM((PLANE, rows, width), full),
            pltpu.VMEM((PLANE, rows, width), full),
            pltpu.VMEM((2, 2, lines - 1, PLANE, rows, width), half),
            pltpu.VMEM((2, 2, lines - 1, PLANE, rows, width), half),
            pltpu.VMEM((2, PLANE, rows, width), half),
            pltpu.VMEM((group, width), full),
            pltpu.VMEM((reps, group, width), full),
            pltpu.VMEM((lines, group, width), full),
            pltpu.VMEM((2, group, width), full),
            pltpu.SMEM((pairs,), jnp.int32),
            pltpu.SMEM((pairs,), jnp.int32),
            pltpu.SMEM((n,), jnp.int32),
            dma((2 + 2 * halves,)),
            dma((2, PLANE - 1)), dma((2, PLANE - 1)),
            dma((2, steps)), dma((2, steps)),
            dma((2, 2, lines - 1)), dma((2, 2, lines - 1)),
            dma((halves,)), dma((steps,)), dma((steps,)),
            dma((2, 2, lines - 1)), dma((2, 2, lines - 1)),
            dma((2,)), dma((2, PLANE - 1)), dma((2, PLANE - 1)),
            dma((reps - 1,)), dma((reps - 1,)),
            dma((lines - 1,)), dma((lines - 1,)),
            dma((PLANE - 1,)), dma((PLANE - 1,)),
        ],
        compiler_params=pltpu.CompilerParams(
            collective_id=1, has_side_effects=True, vmem_limit_bytes=60 * 1024 * 1024
        ),
        name="fused",
    )(lists, counts, bias, q, g, k, v)


def place_kernel(*refs):
    half = len(refs) // 2
    for src, dst in zip(refs[:half], refs[half:]):
        dst[...] = src[...]


def place(*arrays):
    spec = pl.BlockSpec(memory_space=pltpu.VMEM)
    return pl.pallas_call(
        place_kernel,
        in_specs=[spec] * len(arrays),
        out_specs=[spec] * len(arrays),
        out_shape=[jax.ShapeDtypeStruct(one.shape, one.dtype) for one in arrays],
        name="place",
    )(*arrays)


def body(q_lin, k_lin, value_projection, grad_out, q_bias, block_lists, block_counts):
    assert block_lists.shape[1] == lax.axis_size("seq") and block_lists.shape[2] == 2
    heads = block_lists.shape[0]
    dq, dk, dv, dbq = fused(
        jnp.transpose(block_lists, (1, 2, 0)), block_counts.T, q_bias.reshape(heads, -1),
        q_lin[0], grad_out[0], k_lin[0], value_projection[0],
    )
    dq, dk, dv, dbq = place(dq, dk, dv, dbq)
    return (dq[None], dk[None], dv[None], dbq.reshape(-1))


def solution(mesh):
    placed = (P("rep", "seq", None),) * 4 + (P(),) * 3
    return jax.shard_map(
        body,
        mesh=mesh,
        in_specs=placed,
        out_specs=(P("rep", "seq", None),) * 3 + (P(),),
        check_vma=False,
    )
```

time: 123 us -> 69.3 us (0.56)
  Pallas kernels: 115 us -> 68.4 us
  local copies, waits for them, and re-layouts: 5.17 us -> 0 us
    pallas_call x3 -> x2, Pallas kernels: 115 us -> 68.4 us  [the longest x1 66 us: fused(): pl.pallas_call(functools.partial(fused_kernel, group, width ** (-0.5)), i...]
    unnamed x5 -> x0, local copies, waits for them, and re-layouts: 5.17 us -> none
where the time goes in v1:
time: 69.3 us; the launch traced here: 69 us
  Pallas kernels  68.4 us (99%)
    pallas_call x1, Pallas kernels, fused(): pl.pallas_call(functools.partial(fused_kernel, group, width ** (-0.5)), i...  66 us
    pallas_call x1, Pallas kernels, place(): pl.pallas_call(place_kernel, in_specs=[spec] * len(arrays), out_specs=[sp...  2.39 us

profile of v1, /device:TPU:0, one launch (start us, length us, event | category | flops | bytes accessed | tf_op | source)
XLA Modules:
  0.0 69.0 jit_solution(13640597000253159304)
XLA Ops:
  0.6 66.0 %fused.1 = (bf16[128,4096]{1,0:T(8,128)(2,1)}, bf16[128,512]{1,0:T(8,128)(2,1)}, bf16[128,512]{1,0:T(8,128)(2,1)}, f32[32,128]{1,0:T(8,128)}) custom-call(s32[16,2,32]{2,1,0:T(2,128)} %bitcast.15, s32[16,32]{1,0:T(8,128)} %bitcast.17, f32[32,128]{1,0:T(8,128)} %bitcast.16, bf16[128,4096]{1,0:T(8,128)(2,1)} %bitcast.11, bf16[128,4096]{1,0:T(8,128)(2,1)} %bitcast.12, ...), custom_call_target="tpu_custom_call" | custom-call | tf_op jit(solution)/shard_map/fused/pallas_call | solution.py:486
  66.6 2.4 %place.1 = (bf16[128,4096]{1,0:T(8,128)(2,1)}, bf16[128,512]{1,0:T(8,128)(2,1)}, bf16[128,512]{1,0:T(8,128)(2,1)}, f32[32,128]{1,0:T(8,128)}) custom-call(bf16[128,4096]{1,0:T(8,128)(2,1)} %get-tuple-element.12.refs_0_, bf16[128,512]{1,0:T(8,128)(2,1)} %get-tuple-element.13.refs_1_, bf16[128,512]{1,0:T(8,128)(2,1)} %get-tuple-element.14.refs_2_, ...), custom_call_target="tpu_custom_call" | custom-call | tf_op jit(solution)/shard_map/place/pallas_call | solution.py:543

commit v2 on v1

--- a/solution.py
+++ b/solution.py
@@ -23,10 +23,11 @@
     group, scaling,
     lists_ref, count_ref, bias_ref, q_ref, g_ref, k_ref, v_ref,
     dq_ref, dk_ref, dv_ref, dbq_ref,
+    lists_smem, count_smem, bias_buf,
     kall, vall, qbuf, gbuf, dqbuf, weights_buf, chain_k, chain_v, own_k, own_v,
     rs_send, rs_recv, final, bias_acc, rep_slots, z_slots, bias_sums,
     enc_ref, prev_ref, last_ref,
-    local_sem, plane_send, plane_recv, rows_send, rows_recv, z_send, z_recv,
+    table_sem, local_sem, plane_send, plane_recv, rows_send, rows_recv, z_send, z_recv,
     dq_local, dq_send, dq_recv, rs_send_sem, rs_recv_sem,
     out_local, out_send, out_recv, rep_send, rep_recv, zb_send, zb_recv, pb_send, pb_recv,
 ):
@@ -56,21 +57,6 @@
     def cols(start, size):
         return pl.ds(pl.multiple_of(start * width, width), size * width)
 
-    own_kv = [
-        pltpu.make_async_copy(src.at[:, cols(p, 1)], dst.at[me], local_sem.at[a])
-        for a, (src, dst) in enumerate([(k_ref, kall), (v_ref, vall)])
-    ]
-    own_rows = [
-        pltpu.make_async_copy(
-            src.at[:, cols(p * group + hb * UNROLL, UNROLL)], dst.at[hb],
-            local_sem.at[2 + a * halves + hb],
-        )
-        for a, (src, dst) in enumerate([(q_ref, qbuf), (g_ref, gbuf)])
-        for hb in range(halves)
-    ]
-    for copy in own_kv + own_rows:
-        copy.start()
-
     barrier = pltpu.get_barrier_semaphore()
     z_others = [lax.rem(z + d, lines) for d in range(1, lines)]
     rep_others = [lax.rem(rep + d, reps) for d in range(1, reps)]
@@ -80,6 +66,26 @@
         pl.semaphore_signal(barrier, inc=1, device_id=seq(zz, p), device_id_type=MESH)
     for rr in rep_others:
         pl.semaphore_signal(barrier, inc=1, device_id={"rep": rr}, device_id_type=MESH)
+    own_kv = [
+        pltpu.make_async_copy(src.at[:, cols(p, 1)], dst.at[me], local_sem.at[a])
+        for a, (src, dst) in enumerate([(k_ref, kall), (v_ref, vall)])
+    ]
+    own_rows = [
+        pltpu.make_async_copy(
+            src.at[:, cols(p * group + hb * UNROLL, UNROLL)], dst.at[hb],
+            local_sem.at[2 + a * halves + hb],
+        )
+        for a, (src, dst) in enumerate([(q_ref, qbuf), (g_ref, gbuf)])
+        for hb in range(halves)
+    ]
+    tables = [
+        pltpu.make_async_copy(lists_ref, lists_smem, table_sem.at[0]),
+        pltpu.make_async_copy(count_ref, count_smem, table_sem.at[1]),
+    ]
+    bias_copy = pltpu.make_async_copy(bias_ref, bias_buf, table_sem.at[2])
+    for copy in own_kv + tables + own_rows + [bias_copy]:
+        copy.start()
+
     pl.semaphore_wait(barrier, PLANE - 1 + lines - 1 + reps - 1)
 
     def plane_copy(a, s):
@@ -105,62 +111,58 @@
         for it in range(halves, steps):
             rows_copy(a, it).start()
 
-    def z_copy(a, way, d):
-        dst = [kall, vall][a]
-        block = dst.at[pl.ds((z - d if way == 0 else z + d) * PLANE, PLANE)]
-        return remote(
-            block, block, z_send.at[a, way, d], z_recv.at[a, way, d],
+    def z_block(a, place, s):
+        return [kall, vall][a].at[place * PLANE + near(s)]
+
+    def z_copy(a, way, d, s):
+        block = z_block(a, z - d if way == 0 else z + d, s)
+        return remote(
+            block, block, z_send.at[a, way, d, s], z_recv.at[a, way, d, s],
             seq(z + 1 if way == 0 else z - 1, p),
         )
 
-    def z_start(a, d):
-        @pl.when((z + 1 < lines) & (z - d >= 0))
-        def _():
-            z_copy(a, 0, d).start()
-
-        @pl.when((z - 1 >= 0) & (z + d < lines))
-        def _():
-            z_copy(a, 1, d).start()
-
-    def z_arrive(a, d):
-        dst = [kall, vall][a]
-
-        def arrived(way, where):
-            block = dst.at[pl.ds(where * PLANE, PLANE)]
-            remote(
-                block, block, z_send.at[a, way, d - 1], z_recv.at[a, way, d - 1], seq(z, p)
-            ).wait_recv()
-
-        @pl.when(z - d >= 0)
-        def _():
-            arrived(0, z - d)
-
-        @pl.when(z + d < lines)
-        def _():
-            arrived(1, z + d)
-
-    def z_open(a):
-        own_kv[a].wait()
-        for s in range(1, PLANE):
-            plane_copy(a, s).wait_recv()
-        z_start(a, 0)
+    def goes(way, d):
+        if way == 0:
+            return (z + 1 < lines) & (z - d >= 0)
+        return (z - 1 >= 0) & (z + d < lines)
+
+    def goes_any(way):
+        return goes(way, 1)
+
+    def z_start(a, d, s):
+        for way in range(2):
+            @pl.when(goes(way, d))
+            def _():
+                z_copy(a, way, d, s).start()
 
     def z_relay(a, d):
-        z_arrive(a, d)
-        if d < lines - 1:
-            z_start(a, d)
+        for s in range(PLANE):
+            for way in range(2):
+                @pl.when(z - d >= 0 if way == 0 else z + d < lines)
+                def _():
+                    block = z_block(a, z - d if way == 0 else z + d, s)
+                    remote(
+                        block, block, z_send.at[a, way, d - 1, s], z_recv.at[a, way, d - 1, s],
+                        seq(z, p),
+                    ).wait_recv()
+
+            if d < lines - 1:
+                z_start(a, d, s)
+
+    own_kv[0].wait()
+    z_start(0, 0, 0)
+
+    for copy in tables:
+        copy.wait()
 
     def read_table(t, _):
-        s, h = t // group, t % group
-        position = z * PLANE + near(s)
-        head = p * group + h
-        other = jnp.clip(lists_ref[position, 1, head], 0, n - 1)
-        enc_ref[t] = jnp.where(count_ref[position, head] != 1, other, n)
+        position = z * PLANE + near(t // group)
+        head = p * group + t % group
+        other = jnp.clip(lists_smem[position, 1, head], 0, n - 1)
+        enc_ref[t] = jnp.where(count_smem[position, head] != 1, other, n)
         return 0
 
     lax.fori_loop(0, pairs, read_table, 0)
-
-    z_open(0)
 
     def link_pair(t, _):
         code = enc_ref[t]
@@ -171,9 +173,6 @@
         prev_ref[t] = found
         return 0
 
-    lax.fori_loop(0, pairs, link_pair, 0)
-    z_open(1)
-
     def link_block(j, _):
         found = jnp.int32(0)
         for u in range(pairs):
@@ -181,8 +180,20 @@
         last_ref[j] = found
         return 0
 
+    for s in range(1, PLANE):
+        plane_copy(0, s).wait_recv()
+        z_start(0, 0, s)
+    lax.fori_loop(0, pairs, link_pair, 0)
+    own_kv[1].wait()
+    for s in range(PLANE):
+        if s:
+            plane_copy(1, s).wait_recv()
+        for way in range(2):
+            @pl.when(goes(way, 0) & jnp.logical_not(goes_any(way)))
+            def _():
+                z_copy(1, way, 0, s).start()
+
     lax.fori_loop(0, n, link_block, 0)
-
     chain_k[0] = jnp.zeros((rows, width), jnp.float32)
     chain_v[0] = jnp.zeros((rows, width), jnp.float32)
     own_k[...] = jnp.zeros_like(own_k)
@@ -191,8 +202,15 @@
 
     for d in range(1, lines):
         z_relay(0, d)
+    for s in range(PLANE):
+        for way in range(2):
+            @pl.when(goes(way, 0) & goes_any(way))
+            def _():
+                z_copy(1, way, 0, s).start()
+
     for copy in own_rows:
         copy.wait()
+    bias_copy.wait()
 
     def both(ref, it, u):
         t = it * UNROLL + u
@@ -210,7 +228,7 @@
             lanes = slice(u * width, (u + 1) * width)
             head = p * group + (it % halves) * UNROLL + u
             queries = (
-                qbuf[it, :, lanes].astype(jnp.float32) + bias_ref[pl.ds(head, 1), :]
+                qbuf[it, :, lanes].astype(jnp.float32) + bias_buf[pl.ds(head, 1), :]
             ).astype(jnp.bfloat16)
             qbuf[it, :, lanes] = queries
             keys, code = both(kall, it, u)
@@ -310,50 +328,57 @@
     factors = [scaling, 1.0]
     chains = [chain_k, chain_v]
     owns = [own_k, own_v]
-
-    def rs_copy(a, way, d):
-        return remote(
-            rs_send.at[a, way, d - 1], rs_recv.at[a, way, d - 1],
-            rs_send_sem.at[a, way, d - 1], rs_recv_sem.at[a, way, d - 1],
+    order = [3, 1, 2, 0]
+
+    def rs_copy(a, way, d, s):
+        return remote(
+            rs_send.at[a, way, d - 1, s], rs_recv.at[a, way, d - 1, s],
+            rs_send_sem.at[a, way, d - 1, s], rs_recv_sem.at[a, way, d - 1, s],
             seq(z + 1 if way == 0 else z - 1, p),
         )
 
-    def rs_step(a, way, d):
+    def rs_inner(way):
+        return z >= 1 if way == 0 else z + 1 < lines
+
+    def rs_step(a, way, d, s):
         target = z + d if way == 0 else z - d
         inside = target < lines if way == 0 else target >= 0
-        inner = z >= 1 if way == 0 else z + 1 < lines
-
-        def part(j):
-            return chains[a][last_ref[target * PLANE + j]] * factors[a]
+
+        def part():
+            return chains[a][last_ref[target * PLANE + near(s)]] * factors[a]
 
         if d < lines - 1:
-            @pl.when(inside & inner)
+            @pl.when(inside & rs_inner(way))
             def _():
-                rs_copy(a, way, d + 1).wait_recv()
-                for j in range(PLANE):
-                    rs_send[a, way, d - 1, j] = (
-                        part(j) + rs_recv[a, way, d, j].astype(jnp.float32)
-                    ).astype(jnp.bfloat16)
-                rs_copy(a, way, d).start()
-
-            inside = inside & jnp.logical_not(inner)
+                rs_copy(a, way, d + 1, s).wait_recv()
+                rs_send[a, way, d - 1, s] = (
+                    part() + rs_recv[a, way, d, s].astype(jnp.float32)
+                ).astype(jnp.bfloat16)
+                rs_copy(a, way, d, s).start()
+
+            inside = inside & jnp.logical_not(rs_inner(way))
 
         @pl.when(inside)
         def _():
-            for j in range(PLANE):
-                rs_send[a, way, d - 1, j] = part(j).astype(jnp.bfloat16)
-            rs_copy(a, way, d).start()
-
-    rs_step(1, 0, lines - 1)
-    rs_step(1, 1, lines - 1)
-
-    for d in range(1, reps):
-        rep_copy(d).wait_recv()
-    summed = rep_slots[0]
-    for d in range(1, reps):
-        summed = summed + rep_slots[d]
-    bias_sums[0] = summed
-    z_slots[z] = summed
+            rs_send[a, way, d - 1, s] = part().astype(jnp.bfloat16)
+            rs_copy(a, way, d, s).start()
+
+    def out_copy(a, s):
+        return remote(
+            final.at[a, s], [dk_ref, dv_ref][a].at[:, cols(p, 1)],
+            out_send.at[a, s - 1], out_recv.at[a, s - 1], seq(z, near(s)),
+        )
+
+    def out_arrive(a, s):
+        return remote(
+            final.at[a, s], [dk_ref, dv_ref][a].at[:, cols(near(s), 1)],
+            out_send.at[a, s - 1], out_recv.at[a, s - 1], seq(z, near(s)),
+        )
+
+    def out_stay(a):
+        return pltpu.make_async_copy(
+            final.at[a, 0], [dk_ref, dv_ref][a].at[:, cols(p, 1)], out_local.at[a]
+        )
 
     def zb_copy(d):
         return remote(
@@ -361,49 +386,39 @@
             seq(z_others[d - 1], p),
         )
 
-    for d in range(1, lines):
-        zb_copy(d).start()
-
-    for a in (1, 0):
-        for d in range(lines - 1, 0, -1):
-            if a == 0 or d < lines - 1:
-                rs_step(a, 0, d)
-                rs_step(a, 1, d)
-
-    def out_copy(a, s):
-        return remote(
-            final.at[a, near(s)], [dk_ref, dv_ref][a].at[:, cols(p, 1)],
-            out_send.at[a, s - 1], out_recv.at[a, s - 1], seq(z, near(s)),
-        )
-
-    def out_arrive(a, s):
-        return remote(
-            final.at[a, near(s)], [dk_ref, dv_ref][a].at[:, cols(near(s), 1)],
-            out_send.at[a, s - 1], out_recv.at[a, s - 1], seq(z, near(s)),
-        )
-
-    def out_stay(a):
-        return pltpu.make_async_copy(
-            final.at[a, p], [dk_ref, dv_ref][a].at[:, cols(p, 1)], out_local.at[a]
-        )
-
-    for a in (1, 0):
-        base = []
-        for j in range(PLANE):
-            owns[a][j] = (owns[a][j] + chains[a][last_ref[z * PLANE + j]]) * factors[a]
-
-        for way, inner in ((0, z >= 1), (1, z + 1 < lines)):
-            @pl.when(inner)
+    for d in range(lines - 1, 0, -1):
+        for a in (1, 0):
+            for s in order:
+                rs_step(a, 0, d, s)
+                rs_step(a, 1, d, s)
+        if d == lines - 1:
+            for e in range(1, reps):
+                rep_copy(e).wait_recv()
+            summed = rep_slots[0]
+            for e in range(1, reps):
+                summed = summed + rep_slots[e]
+            bias_sums[0] = summed
+            z_slots[z] = summed
+            for e in range(1, lines):
+                zb_copy(e).start()
+
+    def finish(a, s):
+        j = near(s)
+        owns[a][j] = (owns[a][j] + chains[a][last_ref[z * PLANE + j]]) * factors[a]
+        for way in range(2):
+            @pl.when(rs_inner(way))
             def _():
-                rs_copy(a, way, 1).wait_recv()
-                for j in range(PLANE):
-                    owns[a][j] += rs_recv[a, way, 0, j].astype(jnp.float32)
-
-        for j in range(PLANE):
-            final[a, j] = owns[a][j].astype(jnp.bfloat16)
-        for s in (3, 1, 2):
+                rs_copy(a, way, 1, s).wait_recv()
+                owns[a][j] += rs_recv[a, way, 0, s].astype(jnp.float32)
+
+        final[a, s] = owns[a][j].astype(jnp.bfloat16)
+        if s:
             out_copy(a, s).start()
-        out_stay(a).start()
+        else:
+            out_stay(a).start()
+
+    for s in order:
+        finish(1, s)
 
     for d in range(1, lines):
         zb_copy(d).wait_recv()
@@ -411,24 +426,29 @@
     for d in range(1, lines):
         summed = summed + z_slots[d]
     bias_sums[1] = summed
-    mine = pl.ds(pl.multiple_of(p * group, group), group)
-    dbq_ref[mine, :] = summed
+
+    def bias_rows(chip):
+        return dbq_ref.at[pl.ds(pl.multiple_of(chip * group, group), group)]
+
+    bias_stay = pltpu.make_async_copy(bias_sums.at[1], bias_rows(p), table_sem.at[0])
+    bias_stay.start()
 
     def pb_copy(s):
         return remote(
-            bias_sums.at[1], dbq_ref.at[mine], pb_send.at[s - 1], pb_recv.at[s - 1],
+            bias_sums.at[1], bias_rows(p), pb_send.at[s - 1], pb_recv.at[s - 1], seq(z, near(s))
+        )
+
+    def pb_arrive(s):
+        return remote(
+            bias_sums.at[1], bias_rows(near(s)), pb_send.at[s - 1], pb_recv.at[s - 1],
             seq(z, near(s)),
-        )
-
-    def pb_arrive(s):
-        return remote(
-            bias_sums.at[1],
-            dbq_ref.at[pl.ds(pl.multiple_of(near(s) * group, group), group)],
-            pb_send.at[s - 1], pb_recv.at[s - 1], seq(z, near(s)),
         )
 
     for s in range(1, PLANE):
         pb_copy(s).start()
+
+    for s in order:
+        finish(0, s)
 
     for a in range(2):
         for s in range(1, PLANE):
@@ -437,17 +457,16 @@
             rows_copy(a, it).wait_send()
         for way in range(2):
             for d in range(lines - 1):
-                ahead = z + 1 < lines if way == 0 else z >= 1
-                behind = z - d >= 0 if way == 0 else z + d < lines
-
-                @pl.when(ahead & behind)
+                @pl.when(goes(way, d))
                 def _():
-                    z_copy(a, way, d).wait_send()
+                    for s in range(PLANE):
+                        z_copy(a, way, d, s).wait_send()
 
             for d in range(1, lines):
                 @pl.when(z + d < lines if way == 0 else z - d >= 0)
                 def _():
-                    rs_copy(a, way, d).wait_send()
+                    for s in range(PLANE):
+                        rs_copy(a, way, d, s).wait_send()
     for it in range(halves):
         dq_stay(it).wait()
     for it in range(halves, steps):
@@ -462,6 +481,7 @@
         for s in range(1, PLANE):
             out_copy(a, s).wait_send()
             out_arrive(a, s).wait_recv()
+    bias_stay.wait()
     for s in range(1, PLANE):
         pb_copy(s).wait_send()
         pb_arrive(s).wait_recv()
@@ -479,14 +499,16 @@
     steps = PLANE * halves
     pairs = PLANE * group
     half, full = jnp.bfloat16, jnp.float32
-    smem = pl.BlockSpec(memory_space=pltpu.SMEM)
-    vmem = pl.BlockSpec(memory_space=pltpu.VMEM)
     free = pl.BlockSpec(memory_space=pl.ANY)
     dma = pltpu.SemaphoreType.DMA
+    block = rows * width
+    need = 2 * block * (2 * n + 3 * pairs + 32 * (lines - 1) + 8)
+    need += 4 * block * (2 * pairs + 2 * (pairs + 1) + 2 * PLANE)
+    need += 8 * heads * width * (reps + lines)
     return pl.pallas_call(
         functools.partial(fused_kernel, group, width ** (-0.5)),
-        in_specs=[smem, smem, vmem, free, free, free, free],
-        out_specs=[free, free, free, vmem],
+        in_specs=[pl.BlockSpec(memory_space=pltpu.HBM)] * 7,
+        out_specs=[free] * 4,
         out_shape=[
             jax.ShapeDtypeStruct(q.shape, half),
             jax.ShapeDtypeStruct(k.shape, half),
@@ -494,6 +516,9 @@
             jax.ShapeDtypeStruct(bias.shape, full),
         ],
         scratch_shapes=[
+            pltpu.SMEM(lists.shape, lists.dtype),
+            pltpu.SMEM(counts.shape, counts.dtype),
+            pltpu.VMEM(bias.shape, full),
             pltpu.VMEM((n, rows, width), half),
             pltpu.VMEM((n, rows, width), half),
             pltpu.VMEM((steps, rows, UNROLL * width), half),
@@ -514,37 +539,45 @@
             pltpu.SMEM((pairs,), jnp.int32),
             pltpu.SMEM((pairs,), jnp.int32),
             pltpu.SMEM((n,), jnp.int32),
-            dma((2 + 2 * halves,)),
+            dma((3,)), dma((2 + 2 * halves,)),
             dma((2, PLANE - 1)), dma((2, PLANE - 1)),
             dma((2, steps)), dma((2, steps)),
-            dma((2, 2, lines - 1)), dma((2, 2, lines - 1)),
+            dma((2, 2, lines - 1, PLANE)), dma((2, 2, lines - 1, PLANE)),
             dma((halves,)), dma((steps,)), dma((steps,)),
-            dma((2, 2, lines - 1)), dma((2, 2, lines - 1)),
+            dma((2, 2, lines - 1, PLANE)), dma((2, 2, lines - 1, PLANE)),
             dma((2,)), dma((2, PLANE - 1)), dma((2, PLANE - 1)),
             dma((reps - 1,)), dma((reps - 1,)),
             dma((lines - 1,)), dma((lines - 1,)),
             dma((PLANE - 1,)), dma((PLANE - 1,)),
         ],
         compiler_params=pltpu.CompilerParams(
-            collective_id=1, has_side_effects=True, vmem_limit_bytes=60 * 1024 * 1024
+            collective_id=1, has_side_effects=True, vmem_limit_bytes=need + 4 * 2**20
         ),
         name="fused",
     )(lists, counts, bias, q, g, k, v)
 
 
 def place_kernel(*refs):
-    half = len(refs) // 2
-    for src, dst in zip(refs[:half], refs[half:]):
-        dst[...] = src[...]
+    count = len(refs) // 2
+    sem = refs[-1]
+    copies = [
+        pltpu.make_async_copy(refs[a], refs[count + a], sem.at[a]) for a in range(count)
+    ]
+    for copy in copies:
+        copy.start()
+    for copy in copies:
+        copy.wait()
 
 
 def place(*arrays):
-    spec = pl.BlockSpec(memory_space=pltpu.VMEM)
+    spec = pl.BlockSpec(memory_space=pl.ANY)
     return pl.pallas_call(
         place_kernel,
         in_specs=[spec] * len(arrays),
         out_specs=[spec] * len(arrays),
         out_shape=[jax.ShapeDtypeStruct(one.shape, one.dtype) for one in arrays],
+        scratch_shapes=[pltpu.SemaphoreType.DMA((len(arrays),))],
+        compiler_params=pltpu.CompilerParams(vmem_limit_bytes=2**20),
         name="place",
     )(*arrays)
 
@@ -552,10 +585,10 @@
 def body(q_lin, k_lin, value_projection, grad_out, q_bias, block_lists, block_counts):
     assert block_lists.shape[1] == lax.axis_size("seq") and block_lists.shape[2] == 2
     heads = block_lists.shape[0]
-    dq, dk, dv, dbq = fused(
-        jnp.transpose(block_lists, (1, 2, 0)), block_counts.T, q_bias.reshape(heads, -1),
-        q_lin[0], grad_out[0], k_lin[0], value_projection[0],
-    )
+    args = (jnp.transpose(block_lists, (1, 2, 0)), block_counts.T, q_bias.reshape(heads, -1),
+        q_lin[0], grad_out[0], k_lin[0], value_projection[0])
+    args = [pltpu.with_memory_space_constraint(a, pltpu.HBM) for a in args]
+    dq, dk, dv, dbq = fused(*args)
     dq, dk, dv, dbq = place(dq, dk, dv, dbq)
     return (dq[None], dk[None], dv[None], dbq.reshape(-1))
 

time: 69.3 us -> 60.1 us (0.87)
  Pallas kernels: 68.4 us -> 59.3 us
    pallas_call x1, Pallas kernels: 66 us -> 58.2 us  [fused(): pl.pallas_call(functools.partial(fused_kernel, group, width ** (-0.5)), i...]
    pallas_call x1, Pallas kernels: 2.39 us -> 1.08 us  [place(): pl.pallas_call(place_kernel, in_specs=[spec] * len(arrays), out_specs=[sp...]
where the time goes in v2:
time: 60.1 us; the launch traced here: 59.9 us
  Pallas kernels  59.3 us (99%)
  between operations  0.64 us (1%)
    pallas_call x1, Pallas kernels, fused(): pl.pallas_call(functools.partial(fused_kernel, group, width ** (-0.5)), i...  58.2 us

profile of v2, /device:TPU:0, one launch (start us, length us, event | category | flops | bytes accessed | tf_op | source)
XLA Modules:
  0.0 59.9 jit_solution(888380291274206980)
XLA Ops:
  0.6 58.2 %fused.1 = (bf16[128,4096]{1,0:T(8,128)(2,1)S(1)}, bf16[128,512]{1,0:T(8,128)(2,1)S(1)}, bf16[128,512]{1,0:T(8,128)(2,1)S(1)}, f32[32,128]{1,0:T(8,128)S(1)}) custom-call(s32[16,2,32]{2,1,0:T(2,128)} %bitcast.15, s32[16,32]{1,0:T(8,128)} %bitcast.17, f32[32,128]{1,0:T(8,128)} %bitcast.16, bf16[128,4096]{1,0:T(8,128)(2,1)} %bitcast.11, ...), custom_call_target="tpu_custom_call" | custom-call | tf_op jit(solution)/shard_map/fused/pallas_call | solution.py:508
  58.9 1.1 %place.1 = (bf16[128,4096]{1,0:T(8,128)(2,1)}, bf16[128,512]{1,0:T(8,128)(2,1)}, bf16[128,512]{1,0:T(8,128)(2,1)}, f32[32,128]{1,0:T(8,128)}) custom-call(bf16[128,4096]{1,0:T(8,128)(2,1)S(1)} %get-tuple-element.12.refs_0_, bf16[128,512]{1,0:T(8,128)(2,1)S(1)} %get-tuple-element.13.refs_1_, bf16[128,512]{1,0:T(8,128)(2,1)S(1)} %get-tuple-element.14.refs_2_, ...), custom_call_target="tpu_custom_call" | custom-call | tf_op jit(solution)/shard_map/place/pallas_call | solution.py:574

commit v3 on v2

v3 whole, which is shorter than its diff:
```python
import functools

import jax
import jax.numpy as jnp
from jax import lax
from jax.experimental import pallas as pl
from jax.experimental.pallas import tpu as pltpu
from jax.sharding import PartitionSpec as P

NT = (((1,), (1,)), ((), ()))
TN = (((0,), (0,)), ((), ()))
NN = (((1,), (0,)), ((), ()))
MESH = pl.DeviceIdType.MESH
PLANE = 4
PAIR = 2


def dot(a, b, dims):
    return lax.dot_general(a, b, dims, preferred_element_type=jnp.float32)


def fused_kernel(
    group, scaling,
    lists_ref, count_ref, bias_ref, q_ref, g_ref, k_ref, v_ref,
    dq_ref, dk_ref, dv_ref, dbq_ref,
    lists_smem, count_smem, bias_buf,
    kall, vall, qbuf, gbuf, dqbuf, weights_buf, chain_k, chain_v, own_k, own_v,
    rs_send, rs_recv, final, bias_acc, rep_slots, z_slots, bias_sums,
    enc_ref, prev_ref, last_ref,
    table_sem, local_sem, plane_send, plane_recv, rows_send, rows_recv, z_send, z_recv,
    rs_sem, dq_sem, out_sem, rep_send, rep_recv, zb_sem, pb_sem,
):
    me = lax.axis_index("seq")
    n = lax.axis_size("seq")
    reps, rep = lax.axis_size("rep"), lax.axis_index("rep")
    lines = n // PLANE
    z, p = me // PLANE, me % PLANE
    rows, width = kall.shape[1:]
    pairs = PLANE * group

    def near(s):
        return (p // 2 + s // 2) % 2 * 2 + (p % 2 + s % 2) % 2

    def seq(zz, pp):
        return {"seq": zz * PLANE + pp}

    def remote(src, dst, send, recv, target):
        return pltpu.make_async_remote_copy(
            src_ref=src, dst_ref=dst, send_sem=send, recv_sem=recv,
            device_id=target, device_id_type=MESH,
        )

    def cols(start, size):
        return pl.ds(pl.multiple_of(start * width, width), size * width)

    barrier = pltpu.get_barrier_semaphore()
    z_others = [lax.rem(z + d, lines) for d in range(1, lines)]
    rep_others = [lax.rem(rep + d, reps) for d in range(1, reps)]
    for s in range(1, PLANE):
        pl.semaphore_signal(barrier, inc=1, device_id=seq(z, near(s)), device_id_type=MESH)
    for zz in z_others:
        pl.semaphore_signal(barrier, inc=1, device_id=seq(zz, p), device_id_type=MESH)
    for rr in rep_others:
        pl.semaphore_signal(barrier, inc=1, device_id={"rep": rr}, device_id_type=MESH)
    own_kv = [
        pltpu.make_async_copy(src.at[:, cols(p, 1)], dst.at[me], local_sem.at[a])
        for a, (src, dst) in enumerate([(k_ref, kall), (v_ref, vall)])
    ]
    own_rows = [
        pltpu.make_async_copy(src.at[:, cols(p * group, group)], dst.at[0], local_sem.at[2 + a])
        for a, (src, dst) in enumerate([(q_ref, qbuf), (g_ref, gbuf)])
    ]
    tables = [
        pltpu.make_async_copy(lists_ref, lists_smem, table_sem.at[0]),
        pltpu.make_async_copy(count_ref, count_smem, table_sem.at[1]),
    ]
    bias_copy = pltpu.make_async_copy(bias_ref, bias_buf, table_sem.at[2])
    for copy in own_kv + tables + own_rows + [bias_copy]:
        copy.start()

    pl.semaphore_wait(barrier, PLANE - 1 + lines - 1 + reps - 1)

    def plane_copy(a, s):
        src, dst = [(k_ref, kall), (v_ref, vall)][a]
        return remote(
            src.at[:, cols(near(s), 1)], dst.at[me],
            plane_send.at[a], plane_recv.at[a, s - 1], seq(z, near(s)),
        )

    def plane_sent(a):
        blocks = [kall, vall][a].at[pl.ds(0, PLANE - 1)]
        return remote(blocks, blocks, plane_send.at[a], plane_recv.at[a, 0], seq(z, p))

    for a in range(2):
        for s in range(1, PLANE):
            plane_copy(a, s).start()

    def rows_copy(a, s, first=0, count=group):
        src, dst = [(q_ref, qbuf), (g_ref, gbuf)][a]
        which = s - 1 if first == 0 else PLANE - 1
        return remote(
            src.at[:, cols(near(s) * group + first, count)],
            dst.at[s, :, first * width : (first + count) * width],
            rows_send.at[a], rows_recv.at[a, which], seq(z, near(s)),
        )

    def rows_sent(a):
        rows_of = [qbuf, gbuf][a].at[pl.ds(1, PLANE - 1)]
        return remote(rows_of, rows_of, rows_send.at[a], rows_recv.at[a, 0], seq(z, p))

    half_group = group // 2
    last_rows = [(0, half_group), (half_group, group - half_group)]
    for s in range(1, PLANE - 1):
        rows_copy(0, s).start()
    for s in range(1, PLANE - 1):
        rows_copy(1, s).start()
    rows_copy(0, PLANE - 1).start()
    for first, count in last_rows:
        rows_copy(1, PLANE - 1, first, count).start()

    def z_block(a, place, s):
        return [kall, vall][a].at[place * PLANE + near(s)]

    def z_copy(a, way, d, s):
        block = z_block(a, z - d if way == 0 else z + d, s)
        return remote(
            block, block, z_send.at[a, way, d], z_recv.at[a, way, d, s],
            seq(z + 1 if way == 0 else z - 1, p),
        )

    def goes(way, d):
        if way == 0:
            return (z + 1 < lines) & (z - d >= 0)
        return (z - 1 >= 0) & (z + d < lines)

    def goes_any(way):
        return goes(way, 1)

    def z_start(a, d, s):
        for way in range(2):
            @pl.when(goes(way, d))
            def _():
                z_copy(a, way, d, s).start()

    def z_relay(a, d):
        for s in range(PLANE):
            for way in range(2):
                @pl.when(z - d >= 0 if way == 0 else z + d < lines)
                def _():
                    block = z_block(a, z - d if way == 0 else z + d, s)
                    remote(
                        block, block, z_send.at[a, way, d - 1], z_recv.at[a, way, d - 1, s],
                        seq(z, p),
                    ).wait_recv()

            if d < lines - 1:
                z_start(a, d, s)

    own_kv[0].wait()
    z_start(0, 0, 0)

    for copy in tables:
        copy.wait()

    def read_table(t, _):
        position = z * PLANE + near(t // group)
        head = p * group + t % group
        other = jnp.clip(lists_smem[position, 1, head], 0, n - 1)
        enc_ref[t] = jnp.where(count_smem[position, head] != 1, other, n)
        return 0

    lax.fori_loop(0, pairs, read_table, 0)

    def link_pair(t, _):
        code = enc_ref[t]
        found = jnp.int32(0)
        for u in range(pairs):
            same = (enc_ref[u] == code) & (u < t)
            found = jnp.where(same, u + 1, found)
        prev_ref[t] = found
        return 0

    def link_block(j, _):
        found = jnp.int32(0)
        for u in range(pairs):
            found = jnp.where(enc_ref[u] == j, u + 1, found)
        last_ref[j] = found
        return 0

    for s in range(1, PLANE):
        plane_copy(0, s).wait_recv()
        z_start(0, 0, s)
    lax.fori_loop(0, pairs, link_pair, 0)
    own_kv[1].wait()
    for s in range(PLANE):
        if s:
            plane_copy(1, s).wait_recv()
        for way in range(2):
            @pl.when(goes(way, 0) & jnp.logical_not(goes_any(way)))
            def _():
                z_copy(1, way, 0, s).start()

    lax.fori_loop(0, n, link_block, 0)
    chain_k[0] = jnp.zeros((rows, width), jnp.float32)
    chain_v[0] = jnp.zeros((rows, width), jnp.float32)
    own_k[...] = jnp.zeros_like(own_k)
    own_v[...] = jnp.zeros_like(own_v)
    bias_acc[...] = jnp.zeros_like(bias_acc)

    for d in range(1, lines):
        z_relay(0, d)
    for s in range(PLANE):
        for way in range(2):
            @pl.when(goes(way, 0) & goes_any(way))
            def _():
                z_copy(1, way, 0, s).start()

    for copy in own_rows:
        copy.wait()
    bias_copy.wait()

    def both(ref, s, t):
        code = enc_ref[t]
        other = jnp.where(code < n, code, 0)
        return jnp.concatenate([ref[z * PLANE + near(s)], ref[other]], axis=0), code

    def lanes_of(h):
        return slice(h * width, (h + 1) * width)

    def soften(s):
        for h in range(group):
            t, lanes = s * group + h, lanes_of(h)
            queries = (
                qbuf[s, :, lanes].astype(jnp.float32) + bias_buf[pl.ds(p * group + h, 1), :]
            ).astype(jnp.bfloat16)
            qbuf[s, :, lanes] = queries
            keys, code = both(kall, s, t)
            scores = dot(keys, queries, NT) * scaling
            first = scores[:rows]
            second = scores[rows:] + jnp.where(code < n, 0.0, -1.0e30)
            top = jnp.maximum(
                jnp.max(first, axis=0, keepdims=True), jnp.max(second, axis=0, keepdims=True)
            )
            first, second = jnp.exp(first - top), jnp.exp(second - top)
            total = jnp.sum(first, axis=0, keepdims=True) + jnp.sum(second, axis=0, keepdims=True)
            scale_to = 1.0 / total
            weights_buf[t, :rows] = first * scale_to
            weights_buf[t, rows:] = second * scale_to

    def dq_copy(s):
        return remote(
            dqbuf.at[s], dq_ref.at[:, cols(p * group, group)],
            dq_sem.at[0], dq_sem.at[1], seq(z, near(s)),
        )

    dq_stay = pltpu.make_async_copy(dqbuf.at[0], dq_ref.at[:, cols(p * group, group)], dq_sem.at[2])
    others = dqbuf.at[pl.ds(1, PLANE - 1)]
    dq_all = remote(others, others, dq_sem.at[0], dq_sem.at[1], seq(z, p))

    def grad_values(s, heads):
        more_v = None
        for h in heads:
            t = s * group + h
            part_v = dot(weights_buf[t].astype(jnp.bfloat16), gbuf[s, :, lanes_of(h)], NN)
            chain_v[t + 1] = part_v[rows:] + chain_v[prev_ref[t]]
            more_v = part_v[:rows] if more_v is None else more_v + part_v[:rows]
        own_v[s] += more_v

    def grad_keys(s, heads):
        more_k = None
        held = []
        for h in heads:
            values, _ = both(vall, s, s * group + h)
            held.append(dot(values, gbuf[s, :, lanes_of(h)], NT))
        for h, weight_grads in zip(heads, held):
            t, lanes = s * group + h, lanes_of(h)
            keys, _ = both(kall, s, t)
            weights = weights_buf[t]
            half = weights.astype(jnp.bfloat16)
            row_dots = jnp.sum(half.astype(jnp.float32) * weight_grads, axis=0, keepdims=True)
            score_grads = (weights * (weight_grads - row_dots)).astype(jnp.bfloat16)
            grad_q = scaling * dot(score_grads, keys, TN)
            dqbuf[s, :, lanes] = grad_q.astype(jnp.bfloat16)
            bias_acc[h : h + 1, :] += jnp.sum(grad_q, axis=0, keepdims=True)
            part_k = dot(score_grads, qbuf[s, :, lanes], NN)
            chain_k[t + 1] = part_k[rows:] + chain_k[prev_ref[t]]
            more_k = part_k[:rows] if more_k is None else more_k + part_k[:rows]
        own_k[s] += more_k

    every = list(range(group))
    early = []
    for s in range(PLANE - 1):
        early.append((0, s))
        early.append((1, s))
    early.append((0, PLANE - 1))
    cut = [len(early) * d // lines for d in range(lines + 1)]

    def run(kind, s):
        if s:
            rows_copy(kind, s).wait_recv()
        if kind == 0:
            soften(s)
        else:
            grad_values(s, every)

    for d in range(lines):
        if d:
            z_relay(1, d)
        for kind, s in early[cut[d] : cut[d + 1]]:
            run(kind, s)
    for s in range(PLANE - 1):
        grad_keys(s, every)
        if s:
            dq_copy(s).start()
        else:
            dq_stay.start()
    for first, count in last_rows:
        heads = list(range(first, first + count))
        rows_copy(1, PLANE - 1, first, count).wait_recv()
        grad_values(PLANE - 1, heads)
        grad_keys(PLANE - 1, heads)
    dq_copy(PLANE - 1).start()

    rep_slots[rep] = bias_acc[...]

    def sent(a, way, d):
        blocks = [kall, vall][a].at[pl.ds(0, PLANE)]
        return remote(blocks, blocks, z_send.at[a, way, d], z_recv.at[a, way, d, 0], seq(z, p))

    for a in range(2):
        for way in range(2):
            for d in range(lines - 1):
                @pl.when(goes(way, d))
                def _():
                    sent(a, way, d).wait_send()

    def rep_copy(d):
        return remote(
            bias_acc, rep_slots.at[rep], rep_send.at[d - 1], rep_recv.at[d - 1],
            {"rep": rep_others[d - 1]},
        )

    for d in range(1, reps):
        rep_copy(d).start()

    factors = [scaling, 1.0]
    chains = [chain_k, chain_v]
    owns = [own_k, own_v]
    order = range(PLANE - PAIR, -1, -PAIR)

    def rs_copy(a, way, d, first):
        pair = pl.ds(first, PAIR)
        return remote(
            rs_send.at[a, way, d - 1, pair], rs_recv.at[a, way, d - 1, pair],
            z_send.at[a, way, d - 1], rs_sem.at[a, way, d - 1, first // PAIR],
            seq(z + 1 if way == 0 else z - 1, p),
        )

    def rs_inner(way):
        return z >= 1 if way == 0 else z + 1 < lines

    def rs_step(a, way, d, first):
        target = z + d if way == 0 else z - d
        inside = target < lines if way == 0 else target >= 0

        def part(s):
            return chains[a][last_ref[target * PLANE + near(s)]] * factors[a]

        if d < lines - 1:
            @pl.when(inside & rs_inner(way))
            def _():
                rs_copy(a, way, d + 1, first).wait_recv()
                for s in range(first, first + PAIR):
                    rs_send[a, way, d - 1, s] = (
                        part(s) + rs_recv[a, way, d, s].astype(jnp.float32)
                    ).astype(jnp.bfloat16)
                rs_copy(a, way, d, first).start()

            inside = inside & jnp.logical_not(rs_inner(way))

        @pl.when(inside)
        def _():
            for s in range(first, first + PAIR):
                rs_send[a, way, d - 1, s] = part(s).astype(jnp.bfloat16)
            rs_copy(a, way, d, first).start()

    def out_copy(a, s):
        return remote(
            final.at[a, s], [dk_ref, dv_ref][a].at[:, cols(p, 1)],
            out_sem.at[0, a], out_sem.at[1, a], seq(z, near(s)),
        )

    def out_all(a):
        blocks = final.at[a, pl.ds(1, PLANE - 1)]
        return remote(blocks, blocks, out_sem.at[0, a], out_sem.at[1, a], seq(z, p))

    def out_stay(a):
        return pltpu.make_async_copy(
            final.at[a, 0], [dk_ref, dv_ref][a].at[:, cols(p, 1)], out_sem.at[2, a]
        )

    def zb_copy(d):
        return remote(
            bias_sums.at[0], z_slots.at[z], zb_sem.at[0], zb_sem.at[1],
            seq(z_others[d - 1], p),
        )

    slots = z_slots.at[pl.ds(0, lines - 1)]
    zb_all = remote(slots, slots, zb_sem.at[0], zb_sem.at[1], seq(z, p))

    for d in range(lines - 1, 0, -1):
        for a in (1, 0):
            for first in order:
                rs_step(a, 0, d, first)
                rs_step(a, 1, d, first)
        if d == lines - 1:
            for e in range(1, reps):
                rep_copy(e).wait_recv()
            summed = rep_slots[0]
            for e in range(1, reps):
                summed = summed + rep_slots[e]
            bias_sums[0] = summed
            z_slots[z] = summed
            for e in range(1, lines):
                zb_copy(e).start()

    def finish(a, first):
        block = range(first, first + PAIR)
        for s in block:
            owns[a][s] = (owns[a][s] + chains[a][last_ref[z * PLANE + near(s)]]) * factors[a]
        for way in range(2):
            @pl.when(rs_inner(way))
            def _():
                rs_copy(a, way, 1, first).wait_recv()
                for s in block:
                    owns[a][s] += rs_recv[a, way, 0, s].astype(jnp.float32)

        for s in reversed(block):
            final[a, s] = owns[a][s].astype(jnp.bfloat16)
            if s:
                out_copy(a, s).start()
            else:
                out_stay(a).start()

    for s in order:
        finish(1, s)

    zb_all.wait_recv()
    summed = z_slots[0]
    for d in range(1, lines):
        summed = summed + z_slots[d]
    bias_sums[1] = summed

    def bias_rows(chip):
        return dbq_ref.at[pl.ds(pl.multiple_of(chip * group, group), group)]

    bias_stay = pltpu.make_async_copy(bias_sums.at[1], bias_rows(p), table_sem.at[0])
    bias_stay.start()

    def pb_copy(s):
        return remote(
            bias_sums.at[1], bias_rows(p), pb_sem.at[0], pb_sem.at[1], seq(z, near(s))
        )

    shares = bias_buf.at[pl.ds(0, (PLANE - 1) * group)]
    pb_all = remote(shares, shares, pb_sem.at[0], pb_sem.at[1], seq(z, p))
    for s in range(1, PLANE):
        pb_copy(s).start()

    for s in order:
        finish(0, s)

    for a in range(2):
        plane_sent(a).wait_send()
        rows_sent(a).wait_send()
        for way in range(2):
            for d in range(1, lines):
                @pl.when(z + d < lines if way == 0 else z - d >= 0)
                def _():
                    sent(a, way, d - 1).wait_send()
    dq_stay.wait()
    dq_all.wait()
    for d in range(1, reps):
        rep_copy(d).wait_send()
    zb_all.wait_send()
    for a in range(2):
        out_stay(a).wait()
        out_all(a).wait()
    bias_stay.wait()
    pb_all.wait()


def fused(lists, counts, bias, q, g, k, v):
    n, reps = lax.axis_size("seq"), lax.axis_size("rep")
    rows, total = q.shape
    heads, width = bias.shape
    kv_count = k.shape[1] // width
    group = heads // kv_count
    assert n % PLANE == 0 and kv_count == PLANE and group % 2 == 0
    lines = n // PLANE
    pairs = PLANE * group
    half, full = jnp.bfloat16, jnp.float32
    free = pl.BlockSpec(memory_space=pl.ANY)
    dma = pltpu.SemaphoreType.DMA
    block = rows * width
    need = 2 * block * (2 * n + 3 * pairs + 32 * (lines - 1) + 8)
    need += 4 * block * (2 * pairs + 2 * (pairs + 1) + 2 * PLANE)
    need += 8 * heads * width * (reps + lines)
    return pl.pallas_call(
        functools.partial(fused_kernel, group, width ** (-0.5)),
        in_specs=[pl.BlockSpec(memory_space=pltpu.HBM)] * 7,
        out_specs=[free] * 4,
        out_shape=[
            jax.ShapeDtypeStruct(q.shape, half),
            jax.ShapeDtypeStruct(k.shape, half),
            jax.ShapeDtypeStruct(v.shape, half),
            jax.ShapeDtypeStruct(bias.shape, full),
        ],
        scratch_shapes=[
            pltpu.SMEM(lists.shape, lists.dtype),
            pltpu.SMEM(counts.shape, counts.dtype),
            pltpu.VMEM(bias.shape, full),
            pltpu.VMEM((n, rows, width), half),
            pltpu.VMEM((n, rows, width), half),
            pltpu.VMEM((PLANE, rows, group * width), half),
            pltpu.VMEM((PLANE, rows, group * width), half),
            pltpu.VMEM((PLANE, rows, group * width), half),
            pltpu.VMEM((pairs, 2 * rows, rows), full),
            pltpu.VMEM((pairs + 1, rows, width), full),
            pltpu.VMEM((pairs + 1, rows, width), full),
            pltpu.VMEM((PLANE, rows, width), full),
            pltpu.VMEM((PLANE, rows, width), full),
            pltpu.VMEM((2, 2, lines - 1, PLANE, rows, width), half),
            pltpu.VMEM((2, 2, lines - 1, PLANE, rows, width), half),
            pltpu.VMEM((2, PLANE, rows, width), half),
            pltpu.VMEM((group, width), full),
            pltpu.VMEM((reps, group, width), full),
            pltpu.VMEM((lines, group, width), full),
            pltpu.VMEM((2, group, width), full),
            pltpu.SMEM((pairs,), jnp.int32),
            pltpu.SMEM((pairs,), jnp.int32),
            pltpu.SMEM((n,), jnp.int32),
            dma((3,)), dma((4,)),
            dma((2,)), dma((2, PLANE - 1)),
            dma((2,)), dma((2, PLANE)),
            dma((2, 2, lines - 1)), dma((2, 2, lines - 1, PLANE)),
            dma((2, 2, lines - 1, PLANE // PAIR)), dma((3,)), dma((3, 2)),
            dma((reps - 1,)), dma((reps - 1,)),
            dma((2,)), dma((2,)),
        ],
        compiler_params=pltpu.CompilerParams(
            collective_id=1, has_side_effects=True, vmem_limit_bytes=need + 4 * 2**20
        ),
        name="fused",
    )(lists, counts, bias, q, g, k, v)


def place_kernel(*refs):
    count = len(refs) // 2
    sem = refs[-1]
    copies = [
        pltpu.make_async_copy(refs[a], refs[count + a], sem.at[a]) for a in range(count)
    ]
    for copy in copies:
        copy.start()
    for copy in copies:
        copy.wait()


def place(*arrays):
    spec = pl.BlockSpec(memory_space=pl.ANY)
    return pl.pallas_call(
        place_kernel,
        in_specs=[spec] * len(arrays),
        out_specs=[spec] * len(arrays),
        out_shape=[jax.ShapeDtypeStruct(one.shape, one.dtype) for one in arrays],
        scratch_shapes=[pltpu.SemaphoreType.DMA((len(arrays),))],
        compiler_params=pltpu.CompilerParams(vmem_limit_bytes=2**20),
        name="place",
    )(*arrays)


def body(q_lin, k_lin, value_projection, grad_out, q_bias, block_lists, block_counts):
    assert block_lists.shape[1] == lax.axis_size("seq") and block_lists.shape[2] == 2
    heads = block_lists.shape[0]
    args = (jnp.transpose(block_lists, (1, 2, 0)), block_counts.T, q_bias.reshape(heads, -1),
        q_lin[0], grad_out[0], k_lin[0], value_projection[0])
    args = [pltpu.with_memory_space_constraint(a, pltpu.HBM) for a in args]
    dq, dk, dv, dbq = fused(*args)
    dq, dk, dv, dbq = place(dq, dk, dv, dbq)
    return (dq[None], dk[None], dv[None], dbq.reshape(-1))


def solution(mesh):
    placed = (P("rep", "seq", None),) * 4 + (P(),) * 3
    return jax.shard_map(
        body,
        mesh=mesh,
        in_specs=placed,
        out_specs=(P("rep", "seq", None),) * 3 + (P(),),
        check_vma=False,
    )
```

time: 60.1 us -> 57.6 us (0.958)
  Pallas kernels: 59.3 us -> 56.8 us
    pallas_call x1, Pallas kernels: 58.2 us -> 55.7 us  [fused(): pl.pallas_call(functools.partial(fused_kernel, group, width ** (-0.5)), i...]
where the time goes in v3:
time: 57.6 us; the launch traced here: 57.4 us
  Pallas kernels  56.8 us (99%)
  between operations  0.64 us (1%)
    pallas_call x1, Pallas kernels, fused(): pl.pallas_call(functools.partial(fused_kernel, group, width ** (-0.5)), i...  55.7 us

profile of v3, /device:TPU:0, one launch (start us, length us, event | category | flops | bytes accessed | tf_op | source)
XLA Modules:
  0.0 57.4 jit_solution(15489128386772634604)
XLA Ops:
  0.6 55.7 %fused.1 = (bf16[128,4096]{1,0:T(8,128)(2,1)S(1)}, bf16[128,512]{1,0:T(8,128)(2,1)S(1)}, bf16[128,512]{1,0:T(8,128)(2,1)S(1)}, f32[32,128]{1,0:T(8,128)S(1)}) custom-call(s32[16,2,32]{2,1,0:T(2,128)} %bitcast.15, s32[16,32]{1,0:T(8,128)} %bitcast.17, f32[32,128]{1,0:T(8,128)} %bitcast.16, bf16[128,4096]{1,0:T(8,128)(2,1)} %bitcast.11, ...), custom_call_target="tpu_custom_call" | custom-call | tf_op jit(solution)/shard_map/fused/pallas_call | solution.py:509
  56.3 1.1 %place.1 = (bf16[128,4096]{1,0:T(8,128)(2,1)}, bf16[128,512]{1,0:T(8,128)(2,1)}, bf16[128,512]{1,0:T(8,128)(2,1)}, f32[32,128]{1,0:T(8,128)}) custom-call(bf16[128,4096]{1,0:T(8,128)(2,1)S(1)} %get-tuple-element.12.refs_0_, bf16[128,512]{1,0:T(8,128)(2,1)S(1)} %get-tuple-element.13.refs_1_, bf16[128,512]{1,0:T(8,128)(2,1)S(1)} %get-tuple-element.14.refs_2_, ...), custom_call_target="tpu_custom_call" | custom-call | tf_op jit(solution)/shard_map/place/pallas_call | solution.py:572

commit v4 on v3

--- a/solution.py
+++ b/solution.py
@@ -28,7 +28,7 @@
     rs_send, rs_recv, final, bias_acc, rep_slots, z_slots, bias_sums,
     enc_ref, prev_ref, last_ref,
     table_sem, local_sem, plane_send, plane_recv, rows_send, rows_recv, z_send, z_recv,
-    rs_sem, dq_sem, out_sem, rep_send, rep_recv, zb_sem, pb_sem,
+    gate, rs_sem, dq_sem, out_sem, rep_send, rep_recv, zb_sem, pb_sem,
 ):
     me = lax.axis_index("seq")
     n = lax.axis_size("seq")
@@ -91,9 +91,20 @@
         blocks = [kall, vall][a].at[pl.ds(0, PLANE - 1)]
         return remote(blocks, blocks, plane_send.at[a], plane_recv.at[a, 0], seq(z, p))
 
-    for a in range(2):
-        for s in range(1, PLANE):
-            plane_copy(a, s).start()
+    lead = rep % 2 == 0
+    follow = rep % 2 == 1
+
+    def tell_partner():
+        pl.semaphore_signal(
+            gate, inc=1, device_id={"rep": rep // 2 * 2 + 1 - rep % 2}, device_id_type=MESH
+        )
+
+    def plane_start():
+        for a in range(2):
+            for s in range(1, PLANE):
+                plane_copy(a, s).start()
+
+    pl.when(lead)(plane_start)
 
     def rows_copy(a, s, first=0, count=group):
         src, dst = [(q_ref, qbuf), (g_ref, gbuf)][a]
@@ -101,22 +112,26 @@
         return remote(
             src.at[:, cols(near(s) * group + first, count)],
             dst.at[s, :, first * width : (first + count) * width],
-            rows_send.at[a], rows_recv.at[a, which], seq(z, near(s)),
-        )
-
-    def rows_sent(a):
-        rows_of = [qbuf, gbuf][a].at[pl.ds(1, PLANE - 1)]
-        return remote(rows_of, rows_of, rows_send.at[a], rows_recv.at[a, 0], seq(z, p))
+            rows_send.at[a if s < PLANE - 1 or a == 0 else 2], rows_recv.at[a, which],
+            seq(z, near(s)),
+        )
+
+    def rows_sent(which):
+        block = [
+            qbuf.at[pl.ds(1, PLANE - 1)], gbuf.at[pl.ds(1, PLANE - 2)], gbuf.at[PLANE - 1]
+        ][which]
+        remote(block, block, rows_send.at[which], rows_recv.at[0, 0], seq(z, p)).wait_send()
 
     half_group = group // 2
     last_rows = [(0, half_group), (half_group, group - half_group)]
-    for s in range(1, PLANE - 1):
-        rows_copy(0, s).start()
-    for s in range(1, PLANE - 1):
-        rows_copy(1, s).start()
-    rows_copy(0, PLANE - 1).start()
-    for first, count in last_rows:
-        rows_copy(1, PLANE - 1, first, count).start()
+    def rows_start():
+        for s in range(1, PLANE - 1):
+            rows_copy(0, s).start()
+        for s in range(1, PLANE - 1):
+            rows_copy(1, s).start()
+        rows_copy(0, PLANE - 1).start()
+        for first, count in last_rows:
+            rows_copy(1, PLANE - 1, first, count).start()
 
     def z_block(a, place, s):
         return [kall, vall][a].at[place * PLANE + near(s)]
@@ -132,9 +147,6 @@
         if way == 0:
             return (z + 1 < lines) & (z - d >= 0)
         return (z - 1 >= 0) & (z + d < lines)
-
-    def goes_any(way):
-        return goes(way, 1)
 
     def z_start(a, d, s):
         for way in range(2):
@@ -156,8 +168,18 @@
             if d < lines - 1:
                 z_start(a, d, s)
 
+    def z_own(a, s, who, which=None):
+        for way in range(2):
+            wanted = goes(way, 0) & who
+            if which is not None:
+                wanted = wanted & (goes(way, 1) if which else jnp.logical_not(goes(way, 1)))
+
+            @pl.when(wanted)
+            def _():
+                z_copy(a, way, 0, s).start()
+
     own_kv[0].wait()
-    z_start(0, 0, 0)
+    z_own(0, 0, lead)
 
     for copy in tables:
         copy.wait()
@@ -170,6 +192,7 @@
         return 0
 
     lax.fori_loop(0, pairs, read_table, 0)
+    pl.when(lead)(rows_start)
 
     def link_pair(t, _):
         code = enc_ref[t]
@@ -187,19 +210,16 @@
         last_ref[j] = found
         return 0
 
+    lax.fori_loop(0, pairs, link_pair, 0)
+    pl.when(follow)(plane_start)
     for s in range(1, PLANE):
         plane_copy(0, s).wait_recv()
-        z_start(0, 0, s)
-    lax.fori_loop(0, pairs, link_pair, 0)
+        z_own(0, s, lead)
     own_kv[1].wait()
     for s in range(PLANE):
         if s:
             plane_copy(1, s).wait_recv()
-        for way in range(2):
-            @pl.when(goes(way, 0) & jnp.logical_not(goes_any(way)))
-            def _():
-                z_copy(1, way, 0, s).start()
-
+        z_own(1, s, lead, False)
     lax.fori_loop(0, n, link_block, 0)
     chain_k[0] = jnp.zeros((rows, width), jnp.float32)
     chain_v[0] = jnp.zeros((rows, width), jnp.float32)
@@ -207,13 +227,29 @@
     own_v[...] = jnp.zeros_like(own_v)
     bias_acc[...] = jnp.zeros_like(bias_acc)
 
+    @pl.when(follow)
+    def _():
+        pl.semaphore_wait(gate, 1)
+        rows_start()
+
+    for s in range(PLANE):
+        z_own(0, s, follow)
+    for s in range(PLANE):
+        z_own(1, s, follow, False)
     for d in range(1, lines):
+        if d == lines - 1:
+            @pl.when(lead)
+            def _():
+                rows_sent(0)
+                rows_sent(1)
+                tell_partner()
+
         z_relay(0, d)
-    for s in range(PLANE):
-        for way in range(2):
-            @pl.when(goes(way, 0) & goes_any(way))
-            def _():
-                z_copy(1, way, 0, s).start()
+        if d == 1:
+            for s in range(PLANE):
+                z_own(1, s, True, True)
+        else:
+            z_relay(1, d - 1)
 
     for copy in own_rows:
         copy.wait()
@@ -293,7 +329,7 @@
         early.append((0, s))
         early.append((1, s))
     early.append((0, PLANE - 1))
-    cut = [len(early) * d // lines for d in range(lines + 1)]
+    cut = len(early) // 2
 
     def run(kind, s):
         if s:
@@ -303,15 +339,21 @@
         else:
             grad_values(s, every)
 
-    for d in range(lines):
-        if d:
-            z_relay(1, d)
-        for kind, s in early[cut[d] : cut[d + 1]]:
-            run(kind, s)
+    for kind, s in early[:cut]:
+        run(kind, s)
+    z_relay(1, lines - 1)
+    for kind, s in early[cut:]:
+        run(kind, s)
+
+    def dq_start(s):
+        @pl.when(follow)
+        def _():
+            dq_copy(s).start()
+
     for s in range(PLANE - 1):
         grad_keys(s, every)
         if s:
-            dq_copy(s).start()
+            dq_start(s)
         else:
             dq_stay.start()
     for first, count in last_rows:
@@ -319,7 +361,14 @@
         rows_copy(1, PLANE - 1, first, count).wait_recv()
         grad_values(PLANE - 1, heads)
         grad_keys(PLANE - 1, heads)
-    dq_copy(PLANE - 1).start()
+    dq_start(PLANE - 1)
+    rows_sent(2)
+
+    @pl.when(follow)
+    def _():
+        rows_sent(0)
+        rows_sent(1)
+        tell_partner()
 
     rep_slots[rep] = bias_acc[...]
 
@@ -413,16 +462,22 @@
             for first in order:
                 rs_step(a, 0, d, first)
                 rs_step(a, 1, d, first)
-        if d == lines - 1:
-            for e in range(1, reps):
-                rep_copy(e).wait_recv()
-            summed = rep_slots[0]
-            for e in range(1, reps):
-                summed = summed + rep_slots[e]
-            bias_sums[0] = summed
-            z_slots[z] = summed
-            for e in range(1, lines):
-                zb_copy(e).start()
+
+    for e in range(1, reps):
+        rep_copy(e).wait_recv()
+    summed = rep_slots[0]
+    for e in range(1, reps):
+        summed = summed + rep_slots[e]
+    bias_sums[0] = summed
+    z_slots[z] = summed
+    for e in range(1, lines):
+        zb_copy(e).start()
+
+    @pl.when(lead)
+    def _():
+        pl.semaphore_wait(gate, 1)
+        for s in range(1, PLANE):
+            dq_copy(s).start()
 
     def finish(a, first):
         block = range(first, first + PAIR)
@@ -472,7 +527,6 @@
 
     for a in range(2):
         plane_sent(a).wait_send()
-        rows_sent(a).wait_send()
         for way in range(2):
             for d in range(1, lines):
                 @pl.when(z + d < lines if way == 0 else z - d >= 0)
@@ -496,7 +550,7 @@
     heads, width = bias.shape
     kv_count = k.shape[1] // width
     group = heads // kv_count
-    assert n % PLANE == 0 and kv_count == PLANE and group % 2 == 0
+    assert reps % 2 == 0 and n % PLANE == 0 and kv_count == PLANE and group % 2 == 0
     lines = n // PLANE
     pairs = PLANE * group
     half, full = jnp.bfloat16, jnp.float32
@@ -542,8 +596,9 @@
             pltpu.SMEM((n,), jnp.int32),
             dma((3,)), dma((4,)),
             dma((2,)), dma((2, PLANE - 1)),
-            dma((2,)), dma((2, PLANE)),
+            dma((3,)), dma((2, PLANE)),
             dma((2, 2, lines - 1)), dma((2, 2, lines - 1, PLANE)),
+            pltpu.SemaphoreType.REGULAR,
             dma((2, 2, lines - 1, PLANE // PAIR)), dma((3,)), dma((3, 2)),
             dma((reps - 1,)), dma((reps - 1,)),
             dma((2,)), dma((2,)),

time: 57.6 us -> 53.6 us (0.931)
  the two profiles are of different devices: /device:TPU:0 before, /device:TPU:1 now
where the time goes in v4:
time: 53.6 us; the launch traced here: 53.5 us
  Pallas kernels  52.8 us (99%)
  between operations  0.64 us (1%)
    pallas_call x1, Pallas kernels, fused(): pl.pallas_call(functools.partial(fused_kernel, group, width ** (-0.5)), i...  51.8 us
    pallas_call x1, Pallas kernels, place(): pl.pallas_call(place_kernel, in_specs=[spec] * len(arrays), out_specs=[sp...  1.08 us

profile of v4, /device:TPU:1, one launch (start us, length us, event | category | flops | bytes accessed | tf_op | source)
XLA Modules:
  0.0 53.5 jit_solution(9156263051633606745)
XLA Ops:
  0.6 51.8 %fused.1 = (bf16[128,4096]{1,0:T(8,128)(2,1)S(1)}, bf16[128,512]{1,0:T(8,128)(2,1)S(1)}, bf16[128,512]{1,0:T(8,128)(2,1)S(1)}, f32[32,128]{1,0:T(8,128)S(1)}) custom-call(s32[16,2,32]{2,1,0:T(2,128)} %bitcast.15, s32[16,32]{1,0:T(8,128)} %bitcast.17, f32[32,128]{1,0:T(8,128)} %bitcast.16, bf16[128,4096]{1,0:T(8,128)(2,1)} %bitcast.11, ...), custom_call_target="tpu_custom_call" | custom-call | tf_op jit(solution)/shard_map/fused/pallas_call | solution.py:563
  52.4 1.1 %place.1 = (bf16[128,4096]{1,0:T(8,128)(2,1)}, bf16[128,512]{1,0:T(8,128)(2,1)}, bf16[128,512]{1,0:T(8,128)(2,1)}, f32[32,128]{1,0:T(8,128)}) custom-call(bf16[128,4096]{1,0:T(8,128)(2,1)S(1)} %get-tuple-element.12.refs_0_, bf16[128,512]{1,0:T(8,128)(2,1)S(1)} %get-tuple-element.13.refs_1_, bf16[128,512]{1,0:T(8,128)(2,1)S(1)} %get-tuple-element.14.refs_2_, ...), custom_call_target="tpu_custom_call" | custom-call | tf_op jit(solution)/shard_map/place/pallas_call | solution.py:627

commit v5 on v4

--- a/solution.py
+++ b/solution.py
@@ -24,7 +24,7 @@
     lists_ref, count_ref, bias_ref, q_ref, g_ref, k_ref, v_ref,
     dq_ref, dk_ref, dv_ref, dbq_ref,
     lists_smem, count_smem, bias_buf,
-    kall, vall, qbuf, gbuf, dqbuf, weights_buf, chain_k, chain_v, own_k, own_v,
+    kbuf, vbuf, kall, vall, qbuf, gbuf, dqbuf, weights_buf, chain_k, chain_v, own_k, own_v,
     rs_send, rs_recv, final, bias_acc, rep_slots, z_slots, bias_sums,
     enc_ref, prev_ref, last_ref,
     table_sem, local_sem, plane_send, plane_recv, rows_send, rows_recv, z_send, z_recv,
@@ -75,13 +75,17 @@
         pltpu.make_async_copy(count_ref, count_smem, table_sem.at[1]),
     ]
     bias_copy = pltpu.make_async_copy(bias_ref, bias_buf, table_sem.at[2])
-    for copy in own_kv + tables + own_rows + [bias_copy]:
+    ahead = [
+        pltpu.make_async_copy(src, dst, local_sem.at[4 + a])
+        for a, (src, dst) in enumerate([(k_ref, kbuf), (v_ref, vbuf)])
+    ]
+    for copy in ahead + own_kv + tables + own_rows + [bias_copy]:
         copy.start()
 
     pl.semaphore_wait(barrier, PLANE - 1 + lines - 1 + reps - 1)
 
     def plane_copy(a, s):
-        src, dst = [(k_ref, kall), (v_ref, vall)][a]
+        src, dst = [(kbuf, kall), (vbuf, vall)][a]
         return remote(
             src.at[:, cols(near(s), 1)], dst.at[me],
             plane_send.at[a], plane_recv.at[a, s - 1], seq(z, near(s)),
@@ -98,6 +102,9 @@
         pl.semaphore_signal(
             gate, inc=1, device_id={"rep": rep // 2 * 2 + 1 - rep % 2}, device_id_type=MESH
         )
+
+    for copy in ahead:
+        copy.wait()
 
     def plane_start():
         for a in range(2):
@@ -248,7 +255,7 @@
         if d == 1:
             for s in range(PLANE):
                 z_own(1, s, True, True)
-        else:
+        elif d < lines - 1:
             z_relay(1, d - 1)
 
     for copy in own_rows:
@@ -329,7 +336,6 @@
         early.append((0, s))
         early.append((1, s))
     early.append((0, PLANE - 1))
-    cut = len(early) // 2
 
     def run(kind, s):
         if s:
@@ -339,11 +345,12 @@
         else:
             grad_values(s, every)
 
-    for kind, s in early[:cut]:
+    for kind, s in early[:2]:
+        run(kind, s)
+    z_relay(1, lines - 2)
+    for kind, s in early[2:5]:
         run(kind, s)
     z_relay(1, lines - 1)
-    for kind, s in early[cut:]:
-        run(kind, s)
 
     def dq_start(s):
         @pl.when(follow)
@@ -351,11 +358,14 @@
             dq_copy(s).start()
 
     for s in range(PLANE - 1):
+        if s == PLANE - 2:
+            run(*early[5])
         grad_keys(s, every)
         if s:
             dq_start(s)
         else:
             dq_stay.start()
+    run(*early[6])
     for first, count in last_rows:
         heads = list(range(first, first + count))
         rows_copy(1, PLANE - 1, first, count).wait_recv()
@@ -557,7 +567,7 @@
     free = pl.BlockSpec(memory_space=pl.ANY)
     dma = pltpu.SemaphoreType.DMA
     block = rows * width
-    need = 2 * block * (2 * n + 3 * pairs + 32 * (lines - 1) + 8)
+    need = 2 * block * (2 * n + 3 * pairs + 32 * (lines - 1) + 8 + 2 * kv_count)
     need += 4 * block * (2 * pairs + 2 * (pairs + 1) + 2 * PLANE)
     need += 8 * heads * width * (reps + lines)
     return pl.pallas_call(
@@ -574,6 +584,8 @@
             pltpu.SMEM(lists.shape, lists.dtype),
             pltpu.SMEM(counts.shape, counts.dtype),
             pltpu.VMEM(bias.shape, full),
+            pltpu.VMEM(k.shape, half),
+            pltpu.VMEM(v.shape, half),
             pltpu.VMEM((n, rows, width), half),
             pltpu.VMEM((n, rows, width), half),
             pltpu.VMEM((PLANE, rows, group * width), half),
@@ -594,7 +606,7 @@
             pltpu.SMEM((pairs,), jnp.int32),
             pltpu.SMEM((pairs,), jnp.int32),
             pltpu.SMEM((n,), jnp.int32),
-            dma((3,)), dma((4,)),
+            dma((3,)), dma((6,)),
             dma((2,)), dma((2, PLANE - 1)),
             dma((3,)), dma((2, PLANE)),
             dma((2, 2, lines - 1)), dma((2, 2, lines - 1, PLANE)),

time: 53.6 us -> 52.2 us (0.974)
  Pallas kernels: 52.8 us -> 51.4 us
    pallas_call x1, Pallas kernels: 51.8 us -> 50.3 us  [fused(): pl.pallas_call(functools.partial(fused_kernel, group, width ** (-0.5)), i...]
where the time goes in v5:
time: 52.2 us; the launch traced here: 52 us
  Pallas kernels  51.4 us (98%)
  between operations  0.64 us (1%)
    pallas_call x1, Pallas kernels, fused(): pl.pallas_call(functools.partial(fused_kernel, group, width ** (-0.5)), i...  50.3 us
    pallas_call x1, Pallas kernels, place(): pl.pallas_call(place_kernel, in_specs=[spec] * len(arrays), out_specs=[sp...  1.08 us

profile of v5, /device:TPU:1, one launch (start us, length us, event | category | flops | bytes accessed | tf_op | source)
XLA Modules:
  0.0 52.0 jit_solution(11300906682127028280)
XLA Ops:
  0.6 50.3 %fused.1 = (bf16[128,4096]{1,0:T(8,128)(2,1)S(1)}, bf16[128,512]{1,0:T(8,128)(2,1)S(1)}, bf16[128,512]{1,0:T(8,128)(2,1)S(1)}, f32[32,128]{1,0:T(8,128)S(1)}) custom-call(s32[16,2,32]{2,1,0:T(2,128)} %bitcast.15, s32[16,32]{1,0:T(8,128)} %bitcast.17, f32[32,128]{1,0:T(8,128)} %bitcast.16, bf16[128,4096]{1,0:T(8,128)(2,1)} %bitcast.11, ...), custom_call_target="tpu_custom_call" | custom-call | tf_op jit(solution)/shard_map/fused/pallas_call | solution.py:573
  50.9 1.1 %place.1 = (bf16[128,4096]{1,0:T(8,128)(2,1)}, bf16[128,512]{1,0:T(8,128)(2,1)}, bf16[128,512]{1,0:T(8,128)(2,1)}, f32[32,128]{1,0:T(8,128)}) custom-call(bf16[128,4096]{1,0:T(8,128)(2,1)S(1)} %get-tuple-element.12.refs_0_, bf16[128,512]{1,0:T(8,128)(2,1)S(1)} %get-tuple-element.13.refs_1_, bf16[128,512]{1,0:T(8,128)(2,1)S(1)} %get-tuple-element.14.refs_2_, ...), custom_call_target="tpu_custom_call" | custom-call | tf_op jit(solution)/shard_map/place/pallas_call | solution.py:639

commit v6 on v5

--- a/solution.py
+++ b/solution.py
@@ -366,22 +366,6 @@
         else:
             dq_stay.start()
     run(*early[6])
-    for first, count in last_rows:
-        heads = list(range(first, first + count))
-        rows_copy(1, PLANE - 1, first, count).wait_recv()
-        grad_values(PLANE - 1, heads)
-        grad_keys(PLANE - 1, heads)
-    dq_start(PLANE - 1)
-    rows_sent(2)
-
-    @pl.when(follow)
-    def _():
-        rows_sent(0)
-        rows_sent(1)
-        tell_partner()
-
-    rep_slots[rep] = bias_acc[...]
-
     def sent(a, way, d):
         blocks = [kall, vall][a].at[pl.ds(0, PLANE)]
         return remote(blocks, blocks, z_send.at[a, way, d], z_recv.at[a, way, d, 0], seq(z, p))
@@ -392,15 +376,6 @@
                 @pl.when(goes(way, d))
                 def _():
                     sent(a, way, d).wait_send()
-
-    def rep_copy(d):
-        return remote(
-            bias_acc, rep_slots.at[rep], rep_send.at[d - 1], rep_recv.at[d - 1],
-            {"rep": rep_others[d - 1]},
-        )
-
-    for d in range(1, reps):
-        rep_copy(d).start()
 
     factors = [scaling, 1.0]
     chains = [chain_k, chain_v]
@@ -443,6 +418,35 @@
                 rs_send[a, way, d - 1, s] = part(s).astype(jnp.bfloat16)
             rs_copy(a, way, d, first).start()
 
+    for part, (first, count) in enumerate(last_rows):
+        heads = range(first, first + count)
+        rows_copy(1, PLANE - 1, first, count).wait_recv()
+        grad_values(PLANE - 1, heads)
+        if part == len(last_rows) - 1:
+            for block in order:
+                for way in range(2):
+                    rs_step(1, way, lines - 1, block)
+        grad_keys(PLANE - 1, heads)
+    dq_start(PLANE - 1)
+    rows_sent(2)
+
+    @pl.when(follow)
+    def _():
+        rows_sent(0)
+        rows_sent(1)
+        tell_partner()
+
+    rep_slots[rep] = bias_acc[...]
+
+    def rep_copy(d):
+        return remote(
+            bias_acc, rep_slots.at[rep], rep_send.at[d - 1], rep_recv.at[d - 1],
+            {"rep": rep_others[d - 1]},
+        )
+
+    for d in range(1, reps):
+        rep_copy(d).start()
+
     def out_copy(a, s):
         return remote(
             final.at[a, s], [dk_ref, dv_ref][a].at[:, cols(p, 1)],
@@ -469,7 +473,7 @@
 
     for d in range(lines - 1, 0, -1):
         for a in (1, 0):
-            for first in order:
+            for first in order if d < lines - 1 or a == 0 else ():
                 rs_step(a, 0, d, first)
                 rs_step(a, 1, d, first)
 

time: 52.2 us -> 51.9 us (level)
  no operation moved by 1% of the time
where the time goes in v6:
time: 51.9 us; the launch traced here: 51.8 us
  Pallas kernels  51.2 us (99%)
  between operations  0.64 us (1%)
    pallas_call x1, Pallas kernels, fused(): pl.pallas_call(functools.partial(fused_kernel, group, width ** (-0.5)), i...  50.1 us
    pallas_call x1, Pallas kernels, place(): pl.pallas_call(place_kernel, in_specs=[spec] * len(arrays), out_specs=[sp...  1.08 us

profile of v6, /device:TPU:1, one launch (start us, length us, event | category | flops | bytes accessed | tf_op | source)
XLA Modules:
  0.0 51.8 jit_solution(15149487110470735823)
XLA Ops:
  0.6 50.1 %fused.1 = (bf16[128,4096]{1,0:T(8,128)(2,1)S(1)}, bf16[128,512]{1,0:T(8,128)(2,1)S(1)}, bf16[128,512]{1,0:T(8,128)(2,1)S(1)}, f32[32,128]{1,0:T(8,128)S(1)}) custom-call(s32[16,2,32]{2,1,0:T(2,128)} %bitcast.15, s32[16,32]{1,0:T(8,128)} %bitcast.17, f32[32,128]{1,0:T(8,128)} %bitcast.16, bf16[128,4096]{1,0:T(8,128)(2,1)} %bitcast.11, ...), custom_call_target="tpu_custom_call" | custom-call | tf_op jit(solution)/shard_map/fused/pallas_call | solution.py:577
  50.7 1.1 %place.1 = (bf16[128,4096]{1,0:T(8,128)(2,1)}, bf16[128,512]{1,0:T(8,128)(2,1)}, bf16[128,512]{1,0:T(8,128)(2,1)}, f32[32,128]{1,0:T(8,128)}) custom-call(bf16[128,4096]{1,0:T(8,128)(2,1)S(1)} %get-tuple-element.12.refs_0_, bf16[128,512]{1,0:T(8,128)(2,1)S(1)} %get-tuple-element.13.refs_1_, bf16[128,512]{1,0:T(8,128)(2,1)S(1)} %get-tuple-element.14.refs_2_, ...), custom_call_target="tpu_custom_call" | custom-call | tf_op jit(solution)/shard_map/place/pallas_call | solution.py:643

commit v7 on v6

--- a/solution.py
+++ b/solution.py
@@ -143,10 +143,13 @@
     def z_block(a, place, s):
         return [kall, vall][a].at[place * PLANE + near(s)]
 
+    def z_slot(d, s):
+        return d * PLANE + (s if d < lines - 2 else 0)
+
     def z_copy(a, way, d, s):
         block = z_block(a, z - d if way == 0 else z + d, s)
         return remote(
-            block, block, z_send.at[a, way, d], z_recv.at[a, way, d, s],
+            block, block, z_send.at[a, way, d], z_recv.at[a, way, z_slot(d, s)],
             seq(z + 1 if way == 0 else z - 1, p),
         )
 
@@ -162,18 +165,29 @@
                 z_copy(a, way, d, s).start()
 
     def z_relay(a, d):
+        if d == lines - 1:
+            for way in range(2):
+                @pl.when(z - d >= 0 if way == 0 else z + d < lines)
+                def _():
+                    where = z - d if way == 0 else z + d
+                    shard = [kall, vall][a].at[pl.ds(where * PLANE, PLANE)]
+                    remote(
+                        shard, shard, z_send.at[a, way, d - 1], z_recv.at[a, way, z_slot(d - 1, 0)],
+                        seq(z, p),
+                    ).wait_recv()
+
+            return
         for s in range(PLANE):
             for way in range(2):
                 @pl.when(z - d >= 0 if way == 0 else z + d < lines)
                 def _():
                     block = z_block(a, z - d if way == 0 else z + d, s)
                     remote(
-                        block, block, z_send.at[a, way, d - 1], z_recv.at[a, way, d - 1, s],
+                        block, block, z_send.at[a, way, d - 1], z_recv.at[a, way, z_slot(d - 1, s)],
                         seq(z, p),
                     ).wait_recv()
 
-            if d < lines - 1:
-                z_start(a, d, s)
+            z_start(a, d, s)
 
     def z_own(a, s, who, which=None):
         for way in range(2):
@@ -226,7 +240,7 @@
     for s in range(PLANE):
         if s:
             plane_copy(1, s).wait_recv()
-        z_own(1, s, lead, False)
+        z_own(1, s, lead)
     lax.fori_loop(0, n, link_block, 0)
     chain_k[0] = jnp.zeros((rows, width), jnp.float32)
     chain_v[0] = jnp.zeros((rows, width), jnp.float32)
@@ -238,6 +252,7 @@
     def _():
         pl.semaphore_wait(gate, 1)
         rows_start()
+        pl.semaphore_wait(gate, 1)
 
     for s in range(PLANE):
         z_own(0, s, follow)
@@ -254,7 +269,7 @@
         z_relay(0, d)
         if d == 1:
             for s in range(PLANE):
-                z_own(1, s, True, True)
+                z_own(1, s, follow, True)
         elif d < lines - 1:
             z_relay(1, d - 1)
 
@@ -345,6 +360,7 @@
         else:
             grad_values(s, every)
 
+    pl.when(lead)(tell_partner)
     for kind, s in early[:2]:
         run(kind, s)
     z_relay(1, lines - 2)
@@ -368,7 +384,7 @@
     run(*early[6])
     def sent(a, way, d):
         blocks = [kall, vall][a].at[pl.ds(0, PLANE)]
-        return remote(blocks, blocks, z_send.at[a, way, d], z_recv.at[a, way, d, 0], seq(z, p))
+        return remote(blocks, blocks, z_send.at[a, way, d], z_recv.at[a, way, 0], seq(z, p))
 
     for a in range(2):
         for way in range(2):
@@ -421,6 +437,13 @@
     for part, (first, count) in enumerate(last_rows):
         heads = range(first, first + count)
         rows_copy(1, PLANE - 1, first, count).wait_recv()
+        if part == len(last_rows) - 1:
+            @pl.when(follow)
+            def _():
+                for which in range(3):
+                    rows_sent(which)
+                tell_partner()
+
         grad_values(PLANE - 1, heads)
         if part == len(last_rows) - 1:
             for block in order:
@@ -428,13 +451,7 @@
                     rs_step(1, way, lines - 1, block)
         grad_keys(PLANE - 1, heads)
     dq_start(PLANE - 1)
-    rows_sent(2)
-
-    @pl.when(follow)
-    def _():
-        rows_sent(0)
-        rows_sent(1)
-        tell_partner()
+    pl.when(lead)(functools.partial(rows_sent, 2))
 
     rep_slots[rep] = bias_acc[...]
 
@@ -474,8 +491,8 @@
     for d in range(lines - 1, 0, -1):
         for a in (1, 0):
             for first in order if d < lines - 1 or a == 0 else ():
+                rs_step(a, 1, d, first)
                 rs_step(a, 0, d, first)
-                rs_step(a, 1, d, first)
 
     for e in range(1, reps):
         rep_copy(e).wait_recv()
@@ -613,7 +630,7 @@
             dma((3,)), dma((6,)),
             dma((2,)), dma((2, PLANE - 1)),
             dma((3,)), dma((2, PLANE)),
-            dma((2, 2, lines - 1)), dma((2, 2, lines - 1, PLANE)),
+            dma((2, 2, lines - 1)), dma((2, 2, (lines - 2) * PLANE + 1)),
             pltpu.SemaphoreType.REGULAR,
             dma((2, 2, lines - 1, PLANE // PAIR)), dma((3,)), dma((3, 2)),
             dma((reps - 1,)), dma((reps - 1,)),

time: 51.9 us -> 51.8 us (level)
  no operation moved by 1% of the time
where the time goes in v7:
time: 51.8 us; the launch traced here: 51.6 us
  Pallas kernels  51 us (98%)
  between operations  0.64 us (1%)
    pallas_call x1, Pallas kernels, fused(): pl.pallas_call(functools.partial(fused_kernel, group, width ** (-0.5)), i...  49.9 us
    pallas_call x1, Pallas kernels, place(): pl.pallas_call(place_kernel, in_specs=[spec] * len(arrays), out_specs=[sp...  1.08 us

profile of v7, /device:TPU:1, one launch (start us, length us, event | category | flops | bytes accessed | tf_op | source)
XLA Modules:
  0.0 51.6 jit_solution(15958402068282835128)
XLA Ops:
  0.6 49.9 %fused.1 = (bf16[128,4096]{1,0:T(8,128)(2,1)S(1)}, bf16[128,512]{1,0:T(8,128)(2,1)S(1)}, bf16[128,512]{1,0:T(8,128)(2,1)S(1)}, f32[32,128]{1,0:T(8,128)S(1)}) custom-call(s32[16,2,32]{2,1,0:T(2,128)} %bitcast.15, s32[16,32]{1,0:T(8,128)} %bitcast.17, f32[32,128]{1,0:T(8,128)} %bitcast.16, bf16[128,4096]{1,0:T(8,128)(2,1)} %bitcast.11, ...), custom_call_target="tpu_custom_call" | custom-call | tf_op jit(solution)/shard_map/fused/pallas_call | solution.py:594
  50.5 1.1 %place.1 = (bf16[128,4096]{1,0:T(8,128)(2,1)}, bf16[128,512]{1,0:T(8,128)(2,1)}, bf16[128,512]{1,0:T(8,128)(2,1)}, f32[32,128]{1,0:T(8,128)}) custom-call(bf16[128,4096]{1,0:T(8,128)(2,1)S(1)} %get-tuple-element.12.refs_0_, bf16[128,512]{1,0:T(8,128)(2,1)S(1)} %get-tuple-element.13.refs_1_, bf16[128,512]{1,0:T(8,128)(2,1)S(1)} %get-tuple-element.14.refs_2_, ...), custom_call_target="tpu_custom_call" | custom-call | tf_op jit(solution)/shard_map/place/pallas_call | solution.py:660

commit v8 on v7

--- a/solution.py
+++ b/solution.py
@@ -129,7 +129,7 @@
         ][which]
         remote(block, block, rows_send.at[which], rows_recv.at[0, 0], seq(z, p)).wait_send()
 
-    half_group = group // 2
+    half_group = group * 3 // 4
     last_rows = [(0, half_group), (half_group, group - half_group)]
     def rows_start():
         for s in range(1, PLANE - 1):
@@ -581,7 +581,7 @@
     heads, width = bias.shape
     kv_count = k.shape[1] // width
     group = heads // kv_count
-    assert reps % 2 == 0 and n % PLANE == 0 and kv_count == PLANE and group % 2 == 0
+    assert reps % 2 == 0 and n % PLANE == 0 and kv_count == PLANE and group % 4 == 0
     lines = n // PLANE
     pairs = PLANE * group
     half, full = jnp.bfloat16, jnp.float32

time: 51.8 us -> 51.8 us (level)
  no operation moved by 1% of the time
where the time goes in v8:
time: 51.8 us; the launch traced here: 51.6 us
  Pallas kernels  51 us (98%)
  between operations  0.64 us (1%)
    pallas_call x1, Pallas kernels, fused(): pl.pallas_call(functools.partial(fused_kernel, group, width ** (-0.5)), i...  49.9 us
    pallas_call x1, Pallas kernels, place(): pl.pallas_call(place_kernel, in_specs=[spec] * len(arrays), out_specs=[sp...  1.08 us

profile of v8, /device:TPU:1, one launch (start us, length us, event | category | flops | bytes accessed | tf_op | source)
XLA Modules:
  0.0 51.6 jit_solution(7624418355494645915)
XLA Ops:
  0.6 49.9 %fused.1 = (bf16[128,4096]{1,0:T(8,128)(2,1)S(1)}, bf16[128,512]{1,0:T(8,128)(2,1)S(1)}, bf16[128,512]{1,0:T(8,128)(2,1)S(1)}, f32[32,128]{1,0:T(8,128)S(1)}) custom-call(s32[16,2,32]{2,1,0:T(2,128)} %bitcast.15, s32[16,32]{1,0:T(8,128)} %bitcast.17, f32[32,128]{1,0:T(8,128)} %bitcast.16, bf16[128,4096]{1,0:T(8,128)(2,1)} %bitcast.11, ...), custom_call_target="tpu_custom_call" | custom-call | tf_op jit(solution)/shard_map/fused/pallas_call | solution.py:594
  50.5 1.1 %place.1 = (bf16[128,4096]{1,0:T(8,128)(2,1)}, bf16[128,512]{1,0:T(8,128)(2,1)}, bf16[128,512]{1,0:T(8,128)(2,1)}, f32[32,128]{1,0:T(8,128)}) custom-call(bf16[128,4096]{1,0:T(8,128)(2,1)S(1)} %get-tuple-element.12.refs_0_, bf16[128,512]{1,0:T(8,128)(2,1)S(1)} %get-tuple-element.13.refs_1_, bf16[128,512]{1,0:T(8,128)(2,1)S(1)} %get-tuple-element.14.refs_2_, ...), custom_call_target="tpu_custom_call" | custom-call | tf_op jit(solution)/shard_map/place/pallas_call | solution.py:660
